TPU v7x, 32 devices: a whole 2x2x4 slice. The times are simulated.
32 devices in a mesh: section: 4 (over z), dp: 2 (over x), mp: 4 (over y, core).
Axes of the slice: x: 2, y: 2, z: 4, core: 2. Of those that a mesh axis runs over, the one named last changes fastest.
Arguments:
- entrance: bfloat16 [2, 2, 96, 4096], P('dp'), may hold values from -6 to 6
- lengths: int32 [2, 2], P('dp'), may hold values from 24 to 96
- positives: int32 [2], replicated, may hold values from 0 to 1, each once
- norm_gains: float32 [4, 4096], P('section'), may hold values from 0.5 to 1.5
- query_proj: bfloat16 [4, 4096, 2048], P('section', None, 'mp'), may hold values from -0.09375 to 0.09375
- key_proj: bfloat16 [4, 4096, 512], P('section', None, 'mp'), may hold values from -0.09375 to 0.09375
- value_proj: bfloat16 [4, 4096, 512], P('section', None, 'mp'), may hold values from -0.09375 to 0.09375
- out_proj: bfloat16 [4, 2048, 4096], P('section', 'mp'), may hold values from -0.125 to 0.125
Outputs:
- losses: float32 [4, 7], P('section')
- norm_gain_grad: float32 [4, 4096], P('section', ('dp', 'mp'))
- query_proj_grad: float32 [4, 4096, 2048], P('section', 'dp', 'mp')
- key_proj_grad: float32 [4, 4096, 512], P('section', 'dp', 'mp')
- value_proj_grad: float32 [4, 4096, 512], P('section', 'dp', 'mp')
- out_proj_grad: float32 [4, 2048, 4096], P('section', 'mp', 'dp')
Inputs may be any that keep to these rules, and one draw needn't show every extreme that they name: positives is a permutation of the pair indices. `lengths`: tokens at or past a sequence's length are padding.
All inputs are finite; a program needn't handle non-finite values.
Results may differ from a plain program's by a relative error of at most 0.039.
Values may be sent and summed in bfloat16 or wider, within the bound.
A program may use at most 128 MiB of HBM per device.

v0:
```python
import functools

import jax
import jax.numpy as jnp
import numpy as np
from jax import lax
from jax.experimental import pallas as pl
from jax.experimental.pallas import tpu as pltpu
from jax.sharding import PartitionSpec as P

HEAD = 128
WIDTHS = 7


EPSILON = 1e-05
SOFTMAX_TEMPER = 0.05
ROPE_BASE = 500000.0
MESH = pl.DeviceIdType.MESH
ROW_TILE = 16
SUB = 4
F32 = jnp.float32
BF16 = jnp.bfloat16


def contract_rows(left, right):
    return lax.dot_general(
        left, right, (((0,), (0,)), ((), ())), preferred_element_type=jnp.float32
    )


def contract_last(left, right):
    return lax.dot_general(
        left, right, (((left.ndim - 1,), (1,)), ((), ())), preferred_element_type=jnp.float32
    )


def rotary_constants(length):
    half_size = HEAD // 2
    frequencies = ROPE_BASE ** (-np.arange(half_size, dtype=np.float64) * 2.0 / HEAD)
    angles = np.arange(length, dtype=np.float64)[:, None] * frequencies[None, :]
    cosine = np.concatenate([np.cos(angles), np.cos(angles)], axis=1)
    sine = np.concatenate([-np.sin(angles), np.sin(angles)], axis=1)
    return np.stack([cosine, sine]).astype(np.float32)


def mp_place(me, levels):
    bits = [(me // (1 << level)) % 2 for level in range(levels)]
    partners = [me + (1 - 2 * bits[level]) * (1 << level) for level in range(levels)]
    return bits, partners


def rows_at(start, size):
    return pl.ds(pl.multiple_of(start, ROW_TILE), size)


def lanes_at(start, size):
    return pl.ds(pl.multiple_of(start, 128), size)


class Place:
    def __init__(self, direction):
        self.here = lax.axis_index("section")
        self.count = lax.axis_size("section")
        (self.low, self.high), (self.near, self.far) = mp_place(lax.axis_index("mp"), 2)
        self.direction = direction
        if direction > 0:
            self.has_source, self.has_target = self.here > 0, self.here < self.count - 1
        else:
            self.has_source, self.has_target = self.here < self.count - 1, self.here > 0

    def quarter(self, flip_low, flip_high):
        low = 1 - self.low if flip_low else self.low
        high = 1 - self.high if flip_high else self.high
        return (low * 2 + high) * SUB


def send(source, target, sems, slot, **device):
    return pltpu.make_async_remote_copy(
        src_ref=source,
        dst_ref=target,
        send_sem=sems[0].at[slot],
        recv_sem=sems[1].at[slot],
        device_id=device,
        device_id_type=MESH,
    )


def stream_in(place, buf, relay, far, near, consume):
    def near_copy(slot, block):
        return send(buf.at[block], buf.at[block], near, slot, mp=place.near)

    def far_copy(slot, block):
        return send(buf.at[block], buf.at[block], far, slot, mp=place.far)

    own, other = place.quarter(0, 0), place.quarter(0, 1)
    near_own, near_other = place.quarter(1, 0), place.quarter(1, 1)
    for tick in range(SUB + 2):
        if tick < SUB:
            block = own + tick
            send(buf.at[block], buf.at[block], relay, tick, section=place.here).wait_recv()
            far_copy(tick, block).start()
            near_copy(tick, block).start()
        if 1 <= tick <= SUB:
            block = other + tick - 1
            far_copy(tick - 1, block).wait_recv()
            near_copy(SUB + tick - 1, block).start()
        if tick >= 2:
            step = tick - 2
            near_copy(step, near_own + step).wait_recv()
            near_copy(SUB + step, near_other + step).wait_recv()

            def body(part, carry, step=step):
                consume(part * SUB + step)
                return carry

            lax.fori_loop(0, 4, body, 0)
    for step in range(SUB):
        far_copy(step, own + step).wait_send()
        near_copy(step, own + step).wait_send()
        near_copy(SUB + step, other + step).wait_send()


def stream_out(place, part, finish, dest, bufs, relay, far, near):
    near_send, near_got, far_send, far_got, relay_send, prepare = bufs

    def near_copy(slot):
        return send(near_send.at[slot], near_got.at[slot], near, slot, mp=place.near)

    def far_copy(step):
        return send(far_send.at[step], far_got.at[step], far, step, mp=place.far)

    def relay_copy(step):
        return send(
            relay_send.at[step],
            dest.at[place.quarter(0, 0) + step],
            relay,
            step,
            section=place.here + place.direction,
        )

    for flip in (1, 0):
        base = (1 - place.high if flip else place.high) * SUB
        for step in range(SUB):
            near_send[base + step] = part(place.quarter(1, flip) + step).astype(BF16)
            near_copy(base + step).start()
    base = (1 - place.high) * SUB
    for step in range(SUB):
        value = part(place.quarter(0, 1) + step)
        near_copy(base + step).wait_recv()
        far_send[step] = (value + near_got[base + step].astype(F32)).astype(BF16)
        far_copy(step).start()
    base = place.high * SUB
    if prepare is not None:
        prepare()
    for step in range(SUB):
        value = part(place.quarter(0, 0) + step)
        near_copy(base + step).wait_recv()
        value = value + near_got[base + step].astype(F32)
        far_copy(step).wait_recv()
        value = value + far_got[step].astype(F32)
        relay_send[step] = finish(place.quarter(0, 0) + step, value)
        relay_copy(step).start()
    for step in range(SUB):
        far_copy(step).wait_send()
        relay_copy(step).wait_send()
    for slot in range(2 * SUB):
        near_copy(slot).wait_send()


def rotary(values, table, sign):
    turned = pltpu.roll(values, HEAD // 2, axis=1)
    return values * table[0] + turned * (table[1] * sign)


def fold_lanes(values):
    total = values[:, :128]
    for lane in range(1, values.shape[1] // 128):
        total = total + values[:, lane * 128 : (lane + 1) * 128]
    return total


def lane_sum(values):
    return jnp.sum(fold_lanes(values), axis=1, keepdims=True)


def matryoshka(queries, passages, target):
    pairs, width_all = queries.shape
    widths = [width_all >> level for level in range(WIDTHS)]
    bounds = [0] + widths[::-1]
    lane = lax.broadcasted_iota(jnp.int32, (pairs, 128), 1)

    def segment_sums(product):
        sums = []
        for low, high in zip(bounds[:-1], bounds[1:]):
            if high <= 128:
                inside = jnp.logical_and(lane >= low, lane < high)
                piece = jnp.where(inside, product[:, :128], 0.0)
            else:
                piece = fold_lanes(product[:, low:high])
            sums.append(jnp.sum(piece, axis=1, keepdims=True))
        for index in range(1, len(sums)):
            sums[index] = sums[index] + sums[index - 1]
        return sums[::-1]

    query_squares = segment_sums(queries * queries)
    passage_squares = segment_sums(passages * passages)
    dots = [segment_sums(queries * passages[j : j + 1]) for j in range(pairs)]
    losses = []
    mixed = [[] for _ in range(pairs)]
    query_own, passage_own = [], []
    for level, width in enumerate(widths):
        query_inv = lax.rsqrt(query_squares[level] * (1.0 / width) + 1e-06)
        passage_inv = lax.rsqrt(passage_squares[level] * (1.0 / width) + 1e-06)
        factors = [
            query_inv * passage_inv[j : j + 1] * (1.0 / (width * SOFTMAX_TEMPER))
            for j in range(pairs)
        ]
        logits = [dots[j][level] * factors[j] for j in range(pairs)]
        highest = logits[0]
        for j in range(1, pairs):
            highest = jnp.maximum(highest, logits[j])
        powers = [jnp.exp(logits[j] - highest) for j in range(pairs)]
        total = powers[0]
        picked = logits[0] * target[:, 0:1]
        for j in range(1, pairs):
            total = total + powers[j]
            picked = picked + logits[j] * target[:, j : j + 1]
        gap = jnp.log(total) + highest - picked
        losses.append(jnp.sum(gap, axis=0, keepdims=True) * (1.0 / pairs))
        slopes = [
            (powers[j] / total - target[:, j : j + 1]) * (1.0 / pairs) for j in range(pairs)
        ]
        pulls = [slopes[j] * logits[j] for j in range(pairs)]
        row_pull = pulls[0]
        for j in range(1, pairs):
            row_pull = row_pull + pulls[j]
        column_pull = jnp.concatenate(
            [jnp.sum(pulls[j], axis=0, keepdims=True) for j in range(pairs)], axis=0
        )
        for j in range(pairs):
            mixed[j].append(slopes[j] * factors[j])
        query_own.append(row_pull * query_inv * query_inv * (-1.0 / width))
        passage_own.append(column_pull * passage_inv * passage_inv * (-1.0 / width))
    for series in mixed + [query_own, passage_own]:
        for level in range(1, WIDTHS):
            series[level] = series[level] + series[level - 1]
    turned = [
        [
            jnp.concatenate([mixed[j][level][p : p + 1] for j in range(pairs)], axis=0)
            for level in range(WIDTHS)
        ]
        for p in range(pairs)
    ]

    def spread(own, own_rows, weights, rows):
        pieces = []
        low = 0
        while low < width_all:
            inside = [k for k in range(WIDTHS) if low < bounds[k + 1] and low + 128 > bounds[k]]
            high = max(low + 128, bounds[inside[-1] + 1])

            def coefficient(series, inside=inside):
                value = series[WIDTHS - 1 - inside[-1]]
                for k in reversed(inside[:-1]):
                    value = jnp.where(lane < bounds[k + 1], series[WIDTHS - 1 - k], value)
                return value

            def columns(values, low=low, high=high):
                return values[:, low:high]

            piece = coefficient(own) * columns(own_rows)
            for j in range(pairs):
                piece = piece + coefficient(weights[j]) * columns(rows[j : j + 1])
            pieces.append(piece)
            low = high
        return jnp.concatenate(pieces, axis=1)

    return (
        losses,
        spread(query_own, queries, mixed, passages),
        spread(passage_own, passages, turned, queries),
    )


SCRATCH = (
    "head_w", "out_w", "acc", "squares", "inv_ref", "query_ref", "key_ref", "value_ref",
    "prob_ref", "pooled", "slopes", "normed_out", "grad_in", "mix_grad", "row_dots", "gain_part",
    "gain_got", "pool_ref", "near_send", "near_got", "far_send", "far_got", "relay_send",
    "near_send_b", "near_got_b", "far_send_b", "far_got_b", "relay_send_b", "load_sem",
    "enter_sem", "relay_s", "relay_r", "in_far_s", "in_far_r", "in_near_s", "in_near_r",
    "out_far_s", "out_far_r", "out_near_s", "out_near_r", "relay_sb", "relay_rb", "in_far_sb",
    "in_far_rb", "in_near_sb", "in_near_rb", "out_far_sb", "out_far_rb", "out_near_sb",
    "out_near_rb", "pool_s", "pool_r", "normed_s", "normed_r", "mixture_s", "mixture_r",
    "outer_s", "outer_r", "heads_s", "heads_r", "dots_s", "dots_r", "gain_s", "gain_r",
)


def step_kernel(
    lengths,
    positives,
    entrance,
    gain,
    table,
    wq,
    wk,
    wv,
    wo,
    losses_out,
    gain_out,
    normed_all,
    mixture_all,
    outer_all,
    heads_all,
    hidden,
    *scratch,
):
    r = dict(zip(SCRATCH, scratch, strict=True))
    head_w, out_w, acc, squares = r["head_w"], r["out_w"], r["acc"], r["squares"]
    forth, back = Place(1), Place(-1)
    blocks, rows, width = hidden.shape
    width_all = blocks * width
    pair_count = lengths.shape[0]
    seq_count = 2 * pair_count
    length = rows // seq_count
    query_cols, kv_cols = wq.shape[1], wk.shape[1]
    groups = query_cols // HEAD
    dp_me, mp_me = lax.axis_index("dp"), lax.axis_index("mp")
    dp_count, mp_count = lax.axis_size("dp"), lax.axis_size("mp")
    members = dp_count * mp_count
    me = dp_me * mp_count + mp_me
    share = blocks // dp_count
    row_pad = r["row_dots"].shape[2]

    def peer(shift):
        spot = lax.rem(me + shift, members)
        return spot // mp_count, lax.rem(spot, mp_count), spot

    loads = [
        pltpu.make_async_copy(wq, head_w.at[:, :query_cols], r["load_sem"].at[0]),
        pltpu.make_async_copy(
            wk, head_w.at[:, query_cols : query_cols + kv_cols], r["load_sem"].at[1]
        ),
        pltpu.make_async_copy(wv, head_w.at[:, query_cols + kv_cols :], r["load_sem"].at[2]),
        pltpu.make_async_copy(wo, out_w, r["load_sem"].at[3]),
    ]

    def enter(block):
        return pltpu.make_async_copy(
            entrance.at[:, lanes_at(block * width, width)],
            hidden.at[block],
            r["enter_sem"].at[block],
        )

    @pl.when(jnp.logical_not(forth.has_source))
    def _():
        for block in range(blocks):
            enter(block).start()

    for load in loads:
        load.start()
    barrier = pltpu.get_barrier_semaphore()
    for shift in range(1, members):
        to_dp, to_mp, _ = peer(shift)
        pl.semaphore_signal(
            barrier, inc=1, device_id={"dp": to_dp, "mp": to_mp}, device_id_type=MESH
        )

    @pl.when(forth.has_source)
    def _():
        pl.semaphore_signal(
            barrier, inc=1, device_id={"section": forth.here - 1}, device_id_type=MESH
        )

    @pl.when(forth.has_target)
    def _():
        pl.semaphore_signal(
            barrier, inc=1, device_id={"section": forth.here + 1}, device_id_type=MESH
        )

    acc[...] = jnp.zeros_like(acc)
    squares[...] = jnp.zeros_like(squares)
    r["mix_grad"][...] = jnp.zeros_like(r["mix_grad"])
    pool_shape = r["pool_ref"].shape
    column = lax.broadcasted_iota(jnp.int32, pool_shape, 1)
    line = lax.broadcasted_iota(jnp.int32, pool_shape, 0)
    picks = jnp.zeros(pool_shape, F32)
    for seq in range(seq_count):
        inside = jnp.logical_and(
            column >= seq * length, column < seq * length + lengths[seq // 2, seq % 2]
        )
        picks = jnp.where(jnp.logical_and(line == seq, inside), 1.0, picks)
    r["pool_ref"][...] = picks.astype(BF16)
    expected = (
        members - 1 + forth.has_source.astype(jnp.int32) + forth.has_target.astype(jnp.int32)
    )
    pl.semaphore_wait(barrier, expected)

    def gain_at(block):
        return gain[:, lanes_at(block * width, width)]

    def consume(block):
        value = hidden[block].astype(F32)
        squares[...] += fold_lanes(value * value)
        acc[...] += jnp.dot(
            (value * gain_at(block)).astype(BF16),
            head_w[rows_at(block * width, width), :],
            preferred_element_type=F32,
        )

    for load in loads[:3]:
        load.wait()

    @pl.when(forth.has_source)
    def _():
        stream_in(
            forth,
            hidden,
            (r["relay_s"], r["relay_r"]),
            (r["in_far_s"], r["in_far_r"]),
            (r["in_near_s"], r["in_near_r"]),
            consume,
        )

    @pl.when(jnp.logical_not(forth.has_source))
    def _():
        def body(block, carry):
            enter(block).wait()
            consume(block)
            return carry

        lax.fori_loop(0, blocks, body, 0)

    inv_rms = lax.rsqrt(
        jnp.sum(squares[...], axis=1, keepdims=True) * (1.0 / width_all) + EPSILON
    )
    r["inv_ref"][...] = inv_rms
    mixture = mixture_all.at[dp_me]
    for seq in range(seq_count):
        span = slice(seq * length, (seq + 1) * length)
        inverse = inv_rms[span]
        query = jnp.concatenate(
            [
                rotary(acc[span, g * HEAD : (g + 1) * HEAD] * inverse, table, 1.0)
                for g in range(groups)
            ],
            axis=0,
        ).astype(BF16)
        key = rotary(acc[span, query_cols : query_cols + kv_cols] * inverse, table, 1.0)
        key = key.astype(BF16)
        value = (acc[span, query_cols + kv_cols :] * inverse).astype(BF16)
        r["query_ref"][seq] = query
        r["key_ref"][seq] = key
        r["value_ref"][seq] = value
        scores = contract_last(query, key) * HEAD ** (-0.5)
        spot = lax.broadcasted_iota(jnp.int32, scores.shape, 0) % length
        scores = jnp.where(spot >= lax.broadcasted_iota(jnp.int32, scores.shape, 1), scores, -1e30)
        weights = jnp.exp(scores - jnp.max(scores, axis=1, keepdims=True))
        weights = weights / jnp.sum(weights, axis=1, keepdims=True)
        r["prob_ref"][seq] = weights
        mixed = jnp.dot(weights.astype(BF16), value, preferred_element_type=F32).astype(BF16)
        for g in range(groups):
            mixture[span, g * HEAD : (g + 1) * HEAD] = mixed[g * length : (g + 1) * length]
    loads[3].wait()

    def out_columns(block):
        return out_w[:, lanes_at(block * width, width)]

    @pl.when(forth.has_target)
    def _():
        def part(block):
            return jnp.dot(mixture[...], out_columns(block), preferred_element_type=F32)

        def finish(block, total):
            return (hidden[block].astype(F32) + total).astype(BF16)

        stream_out(
            forth,
            part,
            finish,
            hidden,
            (r["near_send"], r["near_got"], r["far_send"], r["far_got"], r["relay_send"], None),
            (r["relay_s"], r["relay_r"]),
            (r["out_far_s"], r["out_far_r"]),
            (r["out_near_s"], r["out_near_r"]),
        )

    pool = r["pool_ref"][...]
    mixture_sum = jnp.dot(pool, mixture[...], preferred_element_type=F32)
    coarse = mixture_sum.astype(BF16)
    fine = (mixture_sum - coarse.astype(F32)).astype(BF16)
    both = jnp.concatenate([coarse, fine], axis=0)
    first = (mp_me == 0).astype(F32)
    pooled = r["pooled"]

    def pool_block(block, carry):
        sums = jnp.dot(both, out_columns(block), preferred_element_type=F32)
        sums = sums[: pool_shape[0]] + sums[pool_shape[0] :]
        sums = sums + first * jnp.dot(pool, hidden[block], preferred_element_type=F32)
        lines = [
            sums[seq : seq + 1] / lengths[seq // 2, seq % 2].astype(F32)
            for seq in range(seq_count)
        ]
        pooled[me, :, lanes_at(block * width, width)] = jnp.concatenate(lines, axis=0)
        return carry

    lax.fori_loop(0, blocks, pool_block, 0)

    def pool_copy(shift):
        to_dp, to_mp, _ = peer(shift)
        return pltpu.make_async_remote_copy(
            src_ref=pooled.at[me],
            dst_ref=pooled.at[me],
            send_sem=r["pool_s"].at[shift],
            recv_sem=r["pool_r"].at[me],
            device_id={"dp": to_dp, "mp": to_mp},
            device_id_type=MESH,
        )

    def pool_arrival(shift):
        from_dp, from_mp, spot = peer(shift)
        return pltpu.make_async_remote_copy(
            src_ref=pooled.at[spot],
            dst_ref=pooled.at[spot],
            send_sem=r["pool_s"].at[shift],
            recv_sem=r["pool_r"].at[spot],
            device_id={"dp": from_dp, "mp": from_mp},
            device_id_type=MESH,
        )

    for shift in range(1, members):
        pool_copy(shift).start()

    def to_owner(source, kind, block):
        return pltpu.make_async_remote_copy(
            src_ref=source.at[block],
            dst_ref=(normed_all if kind == "normed" else outer_all).at[dp_me, lax.rem(block, share)],
            send_sem=r[kind + "_s"].at[block],
            recv_sem=r[kind + "_r"].at[dp_me, lax.rem(block, share)],
            device_id={"dp": block // share},
            device_id_type=MESH,
        )

    def from_member(target, kind, member, step):
        return pltpu.make_async_remote_copy(
            src_ref=target.at[member, step],
            dst_ref=target.at[member, step],
            send_sem=r[kind + "_s"].at[0],
            recv_sem=r[kind + "_r"].at[member, step],
            device_id={"dp": member},
            device_id_type=MESH,
        )

    def whole_copy(target, kind, shift):
        return pltpu.make_async_remote_copy(
            src_ref=target.at[dp_me],
            dst_ref=target.at[dp_me],
            send_sem=r[kind + "_s"].at[shift],
            recv_sem=r[kind + "_r"].at[dp_me],
            device_id={"dp": lax.rem(dp_me + shift, dp_count)},
            device_id_type=MESH,
        )

    def whole_arrival(target, kind, shift):
        member = lax.rem(dp_me + shift, dp_count)
        return pltpu.make_async_remote_copy(
            src_ref=target.at[member],
            dst_ref=target.at[member],
            send_sem=r[kind + "_s"].at[shift],
            recv_sem=r[kind + "_r"].at[member],
            device_id={"dp": member},
            device_id_type=MESH,
        )

    def normed_block(block, carry):
        value = hidden[block].astype(F32) * r["inv_ref"][...] * gain_at(block)
        value = value.astype(BF16)
        mine = block // share == dp_me

        @pl.when(mine)
        def _():
            normed_all[dp_me, lax.rem(block, share)] = value

        @pl.when(jnp.logical_not(mine))
        def _():
            r["normed_out"][block] = value
            to_owner(r["normed_out"], "normed", block).start()

        return carry

    lax.fori_loop(0, blocks, normed_block, 0)
    for shift in range(1, dp_count):
        whole_copy(mixture_all, "mixture", shift).start()

    for shift in range(1, members):
        pool_arrival(shift).wait_recv()
    embedded = []
    for member in range(dp_count):
        total = pooled[member * mp_count]
        for other in range(1, mp_count):
            total = total + pooled[member * mp_count + other]
        embedded.append(total)
    pairs = dp_count * pair_count
    queries = jnp.concatenate(
        [embedded[p // pair_count][2 * (p % pair_count) :][:1] for p in range(pairs)], axis=0
    )
    passages = jnp.concatenate(
        [embedded[p // pair_count][2 * (p % pair_count) + 1 :][:1] for p in range(pairs)], axis=0
    )
    partner = lax.broadcasted_iota(jnp.int32, (pairs, pairs), 1)
    line = lax.broadcasted_iota(jnp.int32, (pairs, pairs), 0)
    target = jnp.zeros((pairs, pairs), F32)
    for p in range(pairs):
        target = jnp.where(jnp.logical_and(line == p, partner == positives[p]), 1.0, target)
    losses, query_slopes, passage_slopes = matryoshka(queries, passages, target)
    lane = lax.broadcasted_iota(jnp.int32, (1, 128), 1)
    packed = jnp.zeros((1, 128), F32)
    for level in range(WIDTHS):
        packed = jnp.where(lane == level, losses[level], packed)
    losses_out[...] = packed[:, :WIDTHS]
    slopes = r["slopes"]
    for p in range(pairs):
        slopes[2 * p] = query_slopes[p : p + 1]
        slopes[2 * p + 1] = passage_slopes[p : p + 1]

    grad_in, mix_grad = r["grad_in"], r["mix_grad"]
    spot = lax.broadcasted_iota(jnp.int32, (length, 1), 0)
    shares = []
    for seq in range(seq_count):
        count = lengths[seq // 2, seq % 2]
        shares.append(jnp.where(spot < count, 1.0, 0.0) / count.astype(F32))

    def upstream(block):
        tokens = jnp.concatenate(
            [
                shares[seq] * slopes[dp_me * seq_count + seq, :, lanes_at(block * width, width)]
                for seq in range(seq_count)
            ],
            axis=0,
        )
        return tokens + grad_in[block].astype(F32)

    def consume_back(block):
        outer = upstream(block).astype(BF16)
        mine = block // share == dp_me

        @pl.when(mine)
        def _():
            outer_all[dp_me, lax.rem(block, share)] = outer

        @pl.when(jnp.logical_not(mine))
        def _():
            r["normed_out"][blocks + block] = outer
            to_owner(r["normed_out"].at[pl.ds(blocks, blocks)], "outer", block).start()

        mix_grad[...] += contract_last(outer, out_columns(block))

    @pl.when(back.has_source)
    def _():
        stream_in(
            back,
            grad_in,
            (r["relay_sb"], r["relay_rb"]),
            (r["in_far_sb"], r["in_far_rb"]),
            (r["in_near_sb"], r["in_near_rb"]),
            consume_back,
        )

    @pl.when(jnp.logical_not(back.has_source))
    def _():
        def body(block, carry):
            grad_in[block] = jnp.zeros((rows, width), BF16)
            consume_back(block)
            return carry

        lax.fori_loop(0, blocks, body, 0)

    head_grads = heads_all.at[dp_me]
    row_dot = []
    for seq in range(seq_count):
        span = slice(seq * length, (seq + 1) * length)
        mixed = jnp.concatenate(
            [mix_grad[span, g * HEAD : (g + 1) * HEAD] for g in range(groups)], axis=0
        ).astype(BF16)
        weights = r["prob_ref"][seq]
        value_grad = contract_rows(weights.astype(BF16), mixed).astype(BF16)
        pulled = contract_last(mixed, r["value_ref"][seq]).astype(BF16).astype(F32)
        score_grad = weights * (pulled - jnp.sum(weights * pulled, axis=1, keepdims=True))
        score_grad = (score_grad * HEAD ** (-0.5)).astype(BF16)
        query_grad = jnp.dot(score_grad, r["key_ref"][seq], preferred_element_type=F32)
        query_grad = query_grad.astype(BF16).astype(F32)
        key_grad = contract_rows(score_grad, r["query_ref"][seq]).astype(BF16).astype(F32)
        pieces = [
            rotary(query_grad[g * length : (g + 1) * length], table, -1.0).astype(BF16)
            for g in range(groups)
        ]
        pieces = pieces + [rotary(key_grad, table, -1.0).astype(BF16), value_grad]
        joined = jnp.concatenate(pieces, axis=1)
        head_grads[span, :] = joined
        row_dot.append(lane_sum(joined.astype(F32) * acc[span, :]))
    for shift in range(1, dp_count):
        whole_copy(heads_all, "heads", shift).start()
    row_dot = jnp.concatenate(row_dot, axis=0)

    def part_back(block):
        value = contract_last(head_grads[...], head_w[rows_at(block * width, width), :])
        scaled = value * (hidden[block].astype(F32) * r["inv_ref"][...])
        r["gain_part"][:, lanes_at(block * width, width)] = jnp.sum(scaled, axis=0, keepdims=True)
        return value

    row_dots = r["row_dots"]

    def dots_copy(shift):
        return pltpu.make_async_remote_copy(
            src_ref=row_dots.at[mp_me],
            dst_ref=row_dots.at[mp_me],
            send_sem=r["dots_s"].at[shift],
            recv_sem=r["dots_r"].at[mp_me],
            device_id={"mp": lax.rem(mp_me + shift, mp_count)},
            device_id_type=MESH,
        )

    def dots_arrival(shift):
        member = lax.rem(mp_me + shift, mp_count)
        return pltpu.make_async_remote_copy(
            src_ref=row_dots.at[member],
            dst_ref=row_dots.at[member],
            send_sem=r["dots_s"].at[shift],
            recv_sem=r["dots_r"].at[member],
            device_id={"mp": member},
            device_id_type=MESH,
        )

    @pl.when(back.has_target)
    def _():
        diagonal = lax.broadcasted_iota(jnp.int32, (rows, row_pad), 0) == lax.broadcasted_iota(
            jnp.int32, (rows, row_pad), 1
        )
        row_dots[mp_me] = jnp.sum(jnp.where(diagonal, row_dot, 0.0), axis=0, keepdims=True)
        for shift in range(1, mp_count):
            dots_copy(shift).start()

        def prepare():
            for shift in range(1, mp_count):
                dots_arrival(shift).wait_recv()
            total = row_dots[0]
            for member in range(1, mp_count):
                total = total + row_dots[member]
            column = lane_sum(jnp.where(diagonal, total, 0.0))
            inverse = r["inv_ref"][...]
            squares[:, :1] = column * inverse * inverse * inverse * (1.0 / width_all)

        def finish(block, total):
            value = upstream(block) + total * gain_at(block) * r["inv_ref"][...]
            return (value - hidden[block].astype(F32) * squares[:, :1]).astype(BF16)

        stream_out(
            back,
            part_back,
            finish,
            grad_in,
            (
                r["near_send_b"],
                r["near_got_b"],
                r["far_send_b"],
                r["far_got_b"],
                r["relay_send_b"],
                prepare,
            ),
            (r["relay_sb"], r["relay_rb"]),
            (r["out_far_sb"], r["out_far_rb"]),
            (r["out_near_sb"], r["out_near_rb"]),
        )
        for shift in range(1, mp_count):
            dots_copy(shift).wait_send()

    @pl.when(jnp.logical_not(back.has_target))
    def _():
        def body(block, carry):
            part_back(block)
            return carry

        lax.fori_loop(0, blocks, body, 0)

    gain_got = r["gain_got"]
    gain_cols = gain_got.shape[2]

    def gain_copy(shift):
        to_dp, to_mp, spot = peer(shift)
        return pltpu.make_async_remote_copy(
            src_ref=r["gain_part"].at[:, lanes_at(spot * gain_cols, gain_cols)],
            dst_ref=gain_got.at[me],
            send_sem=r["gain_s"].at[shift],
            recv_sem=r["gain_r"].at[me],
            device_id={"dp": to_dp, "mp": to_mp},
            device_id_type=MESH,
        )

    def gain_arrival(shift):
        from_dp, from_mp, spot = peer(shift)
        return pltpu.make_async_remote_copy(
            src_ref=gain_got.at[spot],
            dst_ref=gain_got.at[spot],
            send_sem=r["gain_s"].at[shift],
            recv_sem=r["gain_r"].at[spot],
            device_id={"dp": from_dp, "mp": from_mp},
            device_id_type=MESH,
        )

    for shift in range(1, members):
        gain_copy(shift).start()
    total = r["gain_part"][:, lanes_at(me * gain_cols, gain_cols)]
    for shift in range(1, members):
        gain_arrival(shift).wait_recv()
        total = total + gain_got[lax.rem(me + shift, members)]
    gain_out[...] = total

    for shift in range(1, members):
        pool_copy(shift).wait_send()
        gain_copy(shift).wait_send()
    for shift in range(1, dp_count):
        whole_copy(mixture_all, "mixture", shift).wait_send()
        whole_copy(heads_all, "heads", shift).wait_send()
        whole_arrival(mixture_all, "mixture", shift).wait_recv()
        whole_arrival(heads_all, "heads", shift).wait_recv()

    def drain(block, carry):
        @pl.when(block // share != dp_me)
        def _():
            to_owner(r["normed_out"], "normed", block).wait_send()
            to_owner(r["normed_out"].at[pl.ds(blocks, blocks)], "outer", block).wait_send()

        return carry

    lax.fori_loop(0, blocks, drain, 0)
    for shift in range(1, dp_count):
        member = lax.rem(dp_me + shift, dp_count)
        for step in range(share):
            from_member(normed_all, "normed", member, step).wait_recv()
            from_member(outer_all, "outer", member, step).wait_recv()


def step_pass(lengths, positives, entrance, gain, table, wq, wk, wv, wo):
    rows, width_all = entrance.shape
    dp_count, mp_count = lax.axis_size("dp"), lax.axis_size("mp")
    members = dp_count * mp_count
    blocks = mp_count * SUB
    width = width_all // blocks
    share = blocks // dp_count
    seq_count = 2 * lengths.shape[0]
    length = rows // seq_count
    query_cols = wq.shape[1]
    head_cols = query_cols + wk.shape[1] + wv.shape[1]
    stacked = query_cols // HEAD * length
    row_pad = -(-rows // 128) * 128
    pool_rows = -(-seq_count // 16) * 16
    dma = pltpu.SemaphoreType.DMA
    block = (rows, width)
    shapes = dict(
        head_w=((width_all, head_cols), BF16),
        out_w=(wo.shape, BF16),
        acc=((rows, head_cols), F32),
        squares=((rows, 128), F32),
        inv_ref=((rows, 1), F32),
        query_ref=((seq_count, stacked, HEAD), BF16),
        key_ref=((seq_count, length, HEAD), BF16),
        value_ref=((seq_count, length, HEAD), BF16),
        prob_ref=((seq_count, stacked, length), F32),
        pooled=((members, seq_count, width_all), F32),
        slopes=((dp_count * seq_count, 1, width_all), F32),
        normed_out=((2 * blocks, *block), BF16),
        grad_in=((blocks, *block), BF16),
        mix_grad=((rows, query_cols), F32),
        row_dots=((mp_count, 1, row_pad), F32),
        gain_part=((1, width_all), F32),
        gain_got=((members, 1, width_all // members), F32),
        pool_ref=((pool_rows, rows), BF16),
    )
    counts = dict(
        load_sem=(4,),
        enter_sem=(blocks,),
        pool_s=(members,),
        pool_r=(members,),
        normed_s=(blocks,),
        normed_r=(dp_count, share),
        outer_s=(blocks,),
        outer_r=(dp_count, share),
        mixture_s=(dp_count,),
        mixture_r=(dp_count,),
        heads_s=(dp_count,),
        heads_r=(dp_count,),
        dots_s=(mp_count,),
        dots_r=(mp_count,),
        gain_s=(members,),
        gain_r=(members,),
    )
    for tail in ("", "_b"):
        shapes["near_send" + tail] = shapes["near_got" + tail] = ((2 * SUB, *block), BF16)
        shapes["far_send" + tail] = shapes["far_got" + tail] = ((SUB, *block), BF16)
        shapes["relay_send" + tail] = ((SUB, *block), BF16)
    for side in ("s", "r", "sb", "rb"):
        counts["relay_" + side] = counts["in_far_" + side] = counts["out_far_" + side] = (SUB,)
        counts["in_near_" + side] = counts["out_near_" + side] = (2 * SUB,)
    scratch = [
        pltpu.VMEM(*shapes[name]) if name in shapes else dma(counts[name]) for name in SCRATCH
    ]
    vmem = pl.BlockSpec(memory_space=pltpu.VMEM)
    smem = pl.BlockSpec(memory_space=pltpu.SMEM)
    hbm = pl.BlockSpec(memory_space=pltpu.HBM)
    return pl.pallas_call(
        step_kernel,
        out_shape=(
            jax.ShapeDtypeStruct((1, WIDTHS), F32),
            jax.ShapeDtypeStruct((1, width_all // members), F32),
            jax.ShapeDtypeStruct((dp_count, share, *block), BF16),
            jax.ShapeDtypeStruct((dp_count, rows, query_cols), BF16),
            jax.ShapeDtypeStruct((dp_count, share, *block), BF16),
            jax.ShapeDtypeStruct((dp_count, rows, head_cols), BF16),
        ),
        in_specs=[smem, smem, hbm, vmem, vmem, hbm, hbm, hbm, hbm],
        out_specs=(vmem,) * 6,
        scratch_shapes=[pltpu.VMEM((blocks, *block), BF16)] + scratch,
        compiler_params=pltpu.CompilerParams(
            collective_id=0, has_side_effects=True, vmem_limit_bytes=56 * 1024 * 1024
        ),
        name="step_pass",
    )(lengths, positives, entrance, gain, table, wq, wk, wv, wo)


def local(entrance, lengths, positives, norm_gains, query_proj, key_proj, value_proj, out_proj):
    length = entrance.shape[2]
    width_all = entrance.shape[3]
    query_cols = query_proj.shape[2]
    kv_cols = key_proj.shape[2]
    losses, gain_share, normed, mixture, outer, heads = step_pass(
        lengths,
        positives,
        entrance.reshape(-1, width_all),
        norm_gains,
        jnp.asarray(rotary_constants(length)),
        query_proj[0],
        key_proj[0],
        value_proj[0],
        out_proj[0],
    )
    normed = normed.transpose(0, 2, 1, 3).reshape(heads.shape[0] * heads.shape[1], -1)
    outer = outer.transpose(0, 2, 1, 3).reshape(heads.shape[0] * heads.shape[1], -1)
    heads = heads.reshape(normed.shape[0], -1)
    mixture = mixture.reshape(normed.shape[0], -1)
    return (
        losses,
        gain_share,
        contract_rows(normed, heads[:, :query_cols])[None],
        contract_rows(normed, heads[:, query_cols : query_cols + kv_cols])[None],
        contract_rows(normed, heads[:, query_cols + kv_cols :])[None],
        contract_rows(mixture, outer)[None],
    )


def solution(mesh):
    in_specs = (
        P("dp", None, None, None),
        P("dp", None),
        P(),
        P("section", None),
        P("section", None, "mp"),
        P("section", None, "mp"),
        P("section", None, "mp"),
        P("section", "mp", None),
    )
    out_specs = (
        P("section", None),
        P("section", ("dp", "mp")),
        P("section", "dp", "mp"),
        P("section", "dp", "mp"),
        P("section", "dp", "mp"),
        P("section", "mp", "dp"),
    )
    return jax.shard_map(local, mesh=mesh, in_specs=in_specs, out_specs=out_specs, check_vma=False)
```

profile of v0, /device:TPU:0, one launch (start us, length us, event | category | flops | bytes accessed | tf_op | source)
XLA Modules:
  0.0 219.5 jit_solution(16407413686366423955)
XLA Ops:
  0.6 203.2 %step_pass.1 = (f32[1,7]{1,0:T(1,128)}, f32[1,512]{1,0:T(1,128)}, bf16[2,8,192,256]{3,2,1,0:T(8,128)(2,1)}, bf16[2,192,512]{2,1,0:T(8,128)(2,1)}, bf16[2,8,192,2...) custom-call(s32[1,2]{1,0:T(1,128)} %lengths.1, s32[2]{0:T(128)} %positives.1, bf16[192,4096]{1,0:T(8,128)(2,1)} %bitcast.36, ...), custom_call_target="tpu_custom_call" | custom-call | tf_op jit(solution)/shard_map/step_pass/pallas_call | solution.py:909
  203.8 2.3 %copy.15 = bf16[2,192,8,256]{3,2,1,0:T(8,128)(2,1)S(1)} copy(bf16[2,192,8,256]{3,1,2,0:T(8,128)(2,1)} %bitcast.38) | data formatting | bytes 3145728 | tf_op jit(solution)/shard_map/transpose | solution.py:945
  206.1 0.0 copy-start.1
  206.1 0.5 copy.17
  206.6 0.6 copy-done.1
  207.1 1.6 convolution_bitcast_fusion.2
  208.7 0.0 copy-start
  208.7 1.6 convolution_bitcast_fusion.3
  210.3 0.0 copy-done
  210.3 0.9 copy.16
  211.2 0.5 copy.18
  211.7 0.0 copy-start.2
  211.7 3.3 %convolution_bitcast_fusion.1 = f32[1,2048,512]{2,1,0:T(8,128)} fusion(bf16[384,2048]{1,0:T(8,128)(2,1)S(1)} %bitcast.30, bf16[384,768]{1,0:T(8,128)(2,1)S(1)} %bitcast.43), kind=kOutput, calls=%fused_computation.1 | convolution fusion | flops 805306368 | bytes 6160384 | tf_op jit(solution)/shard_map/dot_general | solution.py:26
  215.1 0.0 copy-done.2
  215.1 0.0 copy-start.4
  215.1 0.0 copy-start.3
  215.1 3.3 %convolution_bitcast_fusion = f32[1,512,2048]{2,1,0:T(8,128)} fusion(bf16[384,512]{1,0:T(8,128)(2,1)S(1)} %bitcast.44, bf16[384,2048]{1,0:T(8,128)(2,1)S(1)} %bitcast.33), kind=kOutput, calls=%fused_computation | convolution fusion | flops 805306368 | bytes 6160384 | tf_op jit(solution)/shard_map/dot_general | solution.py:26
  218.4 0.0 copy-done.4
  218.4 0.5 copy.21
  218.9 0.0 copy-done.3
  218.9 0.6 copy.22
Async XLA Ops:
  206.1 1.1 copy-start.1
  208.7 1.6 copy-start
  211.7 3.3 %copy-start.2 = (bf16[2,192,512]{2,1,0:T(8,128)(2,1)S(1)}, bf16[2,192,512]{2,1,0:T(8,128)(2,1)}, u32[]{:S(2)}) copy-start(bf16[2,192,512]{2,1,0:T(8,128)(2,1)} %get-tuple-element.16) | copy-start | bytes 1179652
  215.1 3.3 %copy-start.4 = (f32[1,7]{1,0:T(1,128)S(1)}, f32[1,7]{1,0:T(1,128)}, u32[]{:S(2)}) copy-start(f32[1,7]{1,0:T(1,128)} %get-tuple-element.24) | copy-start | bytes 88
  215.1 3.8 %copy-start.3 = (f32[1,512]{1,0:T(1,128)S(1)}, f32[1,512]{1,0:T(1,128)}, u32[]{:S(2)}) copy-start(f32[1,512]{1,0:T(1,128)} %get-tuple-element.25) | copy-start | bytes 6148
where the time goes:
time: 220 us; the launch traced here: 219 us
  Pallas kernels  203 us (92%)
  matrix products  9.81 us (4%)
  local copies, waits for them, and re-layouts  5.82 us (3%)
    pallas_call x1, Pallas kernels, step_pass(): pl.pallas_call(step_kernel, out_shape=(jax.ShapeDtypeStruct((1, WIDTHS),...  203 us
    dot_general x4, matrix products, contract_rows(): lax.dot_general(left, right, (((0,), (0,)), ((), ())), preferred_element_...  9.81 us

commit v1 on v0

--- a/solution.py
+++ b/solution.py
@@ -1,4 +1,4 @@
-import functools
+from typing import NamedTuple
 
 import jax
 import jax.numpy as jnp
@@ -282,17 +282,72 @@
     )
 
 
-SCRATCH = (
-    "head_w", "out_w", "acc", "squares", "inv_ref", "query_ref", "key_ref", "value_ref",
-    "prob_ref", "pooled", "slopes", "normed_out", "grad_in", "mix_grad", "row_dots", "gain_part",
-    "gain_got", "pool_ref", "near_send", "near_got", "far_send", "far_got", "relay_send",
-    "near_send_b", "near_got_b", "far_send_b", "far_got_b", "relay_send_b", "load_sem",
-    "enter_sem", "relay_s", "relay_r", "in_far_s", "in_far_r", "in_near_s", "in_near_r",
-    "out_far_s", "out_far_r", "out_near_s", "out_near_r", "relay_sb", "relay_rb", "in_far_sb",
-    "in_far_rb", "in_near_sb", "in_near_rb", "out_far_sb", "out_far_rb", "out_near_sb",
-    "out_near_rb", "pool_s", "pool_r", "normed_s", "normed_r", "mixture_s", "mixture_r",
-    "outer_s", "outer_r", "heads_s", "heads_r", "dots_s", "dots_r", "gain_s", "gain_r",
-)
+class Scratch(NamedTuple):
+    head_w: object
+    out_w: object
+    acc: object
+    squares: object
+    inv_ref: object
+    query_ref: object
+    key_ref: object
+    value_ref: object
+    prob_ref: object
+    pooled: object
+    slopes: object
+    normed_out: object
+    outer_out: object
+    grad_in: object
+    mix_grad: object
+    row_dots: object
+    gain_part: object
+    gain_got: object
+    pool_ref: object
+    near_send: object
+    near_got: object
+    far_send: object
+    far_got: object
+    relay_send: object
+    near_send_b: object
+    near_got_b: object
+    far_send_b: object
+    far_got_b: object
+    relay_send_b: object
+    load_sem: object
+    enter_sem: object
+    relay_s: object
+    relay_r: object
+    in_far_s: object
+    in_far_r: object
+    in_near_s: object
+    in_near_r: object
+    out_far_s: object
+    out_far_r: object
+    out_near_s: object
+    out_near_r: object
+    relay_sb: object
+    relay_rb: object
+    in_far_sb: object
+    in_far_rb: object
+    in_near_sb: object
+    in_near_rb: object
+    out_far_sb: object
+    out_far_rb: object
+    out_near_sb: object
+    out_near_rb: object
+    pool_s: object
+    pool_r: object
+    normed_s: object
+    normed_r: object
+    mixture_s: object
+    mixture_r: object
+    outer_s: object
+    outer_r: object
+    heads_s: object
+    heads_r: object
+    dots_s: object
+    dots_r: object
+    gain_s: object
+    gain_r: object
 
 
 def step_kernel(
@@ -314,8 +369,8 @@
     hidden,
     *scratch,
 ):
-    r = dict(zip(SCRATCH, scratch, strict=True))
-    head_w, out_w, acc, squares = r["head_w"], r["out_w"], r["acc"], r["squares"]
+    r = Scratch(*scratch)
+    head_w, out_w, acc, squares = r.head_w, r.out_w, r.acc, r.squares
     forth, back = Place(1), Place(-1)
     blocks, rows, width = hidden.shape
     width_all = blocks * width
@@ -329,26 +384,29 @@
     members = dp_count * mp_count
     me = dp_me * mp_count + mp_me
     share = blocks // dp_count
-    row_pad = r["row_dots"].shape[2]
+    row_pad = r.row_dots.shape[2]
+    normed_sems, outer_sems = (r.normed_s, r.normed_r), (r.outer_s, r.outer_r)
+    mixture_sems, heads_sems = (r.mixture_s, r.mixture_r), (r.heads_s, r.heads_r)
+    outer_out = r.outer_out
 
     def peer(shift):
         spot = lax.rem(me + shift, members)
         return spot // mp_count, lax.rem(spot, mp_count), spot
 
     loads = [
-        pltpu.make_async_copy(wq, head_w.at[:, :query_cols], r["load_sem"].at[0]),
+        pltpu.make_async_copy(wq, head_w.at[:, :query_cols], r.load_sem.at[0]),
         pltpu.make_async_copy(
-            wk, head_w.at[:, query_cols : query_cols + kv_cols], r["load_sem"].at[1]
+            wk, head_w.at[:, query_cols : query_cols + kv_cols], r.load_sem.at[1]
         ),
-        pltpu.make_async_copy(wv, head_w.at[:, query_cols + kv_cols :], r["load_sem"].at[2]),
-        pltpu.make_async_copy(wo, out_w, r["load_sem"].at[3]),
+        pltpu.make_async_copy(wv, head_w.at[:, query_cols + kv_cols :], r.load_sem.at[2]),
+        pltpu.make_async_copy(wo, out_w, r.load_sem.at[3]),
     ]
 
     def enter(block):
         return pltpu.make_async_copy(
             entrance.at[:, lanes_at(block * width, width)],
             hidden.at[block],
-            r["enter_sem"].at[block],
+            r.enter_sem.at[block],
         )
 
     @pl.when(jnp.logical_not(forth.has_source))
@@ -379,8 +437,8 @@
 
     acc[...] = jnp.zeros_like(acc)
     squares[...] = jnp.zeros_like(squares)
-    r["mix_grad"][...] = jnp.zeros_like(r["mix_grad"])
-    pool_shape = r["pool_ref"].shape
+    r.mix_grad[...] = jnp.zeros_like(r.mix_grad)
+    pool_shape = r.pool_ref.shape
     column = lax.broadcasted_iota(jnp.int32, pool_shape, 1)
     line = lax.broadcasted_iota(jnp.int32, pool_shape, 0)
     picks = jnp.zeros(pool_shape, F32)
@@ -389,7 +447,7 @@
             column >= seq * length, column < seq * length + lengths[seq // 2, seq % 2]
         )
         picks = jnp.where(jnp.logical_and(line == seq, inside), 1.0, picks)
-    r["pool_ref"][...] = picks.astype(BF16)
+    r.pool_ref[...] = picks.astype(BF16)
     expected = (
         members - 1 + forth.has_source.astype(jnp.int32) + forth.has_target.astype(jnp.int32)
     )
@@ -415,9 +473,9 @@
         stream_in(
             forth,
             hidden,
-            (r["relay_s"], r["relay_r"]),
-            (r["in_far_s"], r["in_far_r"]),
-            (r["in_near_s"], r["in_near_r"]),
+            (r.relay_s, r.relay_r),
+            (r.in_far_s, r.in_far_r),
+            (r.in_near_s, r.in_near_r),
             consume,
         )
 
@@ -433,7 +491,7 @@
     inv_rms = lax.rsqrt(
         jnp.sum(squares[...], axis=1, keepdims=True) * (1.0 / width_all) + EPSILON
     )
-    r["inv_ref"][...] = inv_rms
+    r.inv_ref[...] = inv_rms
     mixture = mixture_all.at[dp_me]
     for seq in range(seq_count):
         span = slice(seq * length, (seq + 1) * length)
@@ -448,15 +506,15 @@
         key = rotary(acc[span, query_cols : query_cols + kv_cols] * inverse, table, 1.0)
         key = key.astype(BF16)
         value = (acc[span, query_cols + kv_cols :] * inverse).astype(BF16)
-        r["query_ref"][seq] = query
-        r["key_ref"][seq] = key
-        r["value_ref"][seq] = value
+        r.query_ref[seq] = query
+        r.key_ref[seq] = key
+        r.value_ref[seq] = value
         scores = contract_last(query, key) * HEAD ** (-0.5)
         spot = lax.broadcasted_iota(jnp.int32, scores.shape, 0) % length
         scores = jnp.where(spot >= lax.broadcasted_iota(jnp.int32, scores.shape, 1), scores, -1e30)
         weights = jnp.exp(scores - jnp.max(scores, axis=1, keepdims=True))
         weights = weights / jnp.sum(weights, axis=1, keepdims=True)
-        r["prob_ref"][seq] = weights
+        r.prob_ref[seq] = weights
         mixed = jnp.dot(weights.astype(BF16), value, preferred_element_type=F32).astype(BF16)
         for g in range(groups):
             mixture[span, g * HEAD : (g + 1) * HEAD] = mixed[g * length : (g + 1) * length]
@@ -478,19 +536,19 @@
             part,
             finish,
             hidden,
-            (r["near_send"], r["near_got"], r["far_send"], r["far_got"], r["relay_send"], None),
-            (r["relay_s"], r["relay_r"]),
-            (r["out_far_s"], r["out_far_r"]),
-            (r["out_near_s"], r["out_near_r"]),
-        )
-
-    pool = r["pool_ref"][...]
+            (r.near_send, r.near_got, r.far_send, r.far_got, r.relay_send, None),
+            (r.relay_s, r.relay_r),
+            (r.out_far_s, r.out_far_r),
+            (r.out_near_s, r.out_near_r),
+        )
+
+    pool = r.pool_ref[...]
     mixture_sum = jnp.dot(pool, mixture[...], preferred_element_type=F32)
     coarse = mixture_sum.astype(BF16)
     fine = (mixture_sum - coarse.astype(F32)).astype(BF16)
     both = jnp.concatenate([coarse, fine], axis=0)
     first = (mp_me == 0).astype(F32)
-    pooled = r["pooled"]
+    pooled = r.pooled
 
     def pool_block(block, carry):
         sums = jnp.dot(both, out_columns(block), preferred_element_type=F32)
@@ -510,8 +568,8 @@
         return pltpu.make_async_remote_copy(
             src_ref=pooled.at[me],
             dst_ref=pooled.at[me],
-            send_sem=r["pool_s"].at[shift],
-            recv_sem=r["pool_r"].at[me],
+            send_sem=r.pool_s.at[shift],
+            recv_sem=r.pool_r.at[me],
             device_id={"dp": to_dp, "mp": to_mp},
             device_id_type=MESH,
         )
@@ -521,8 +579,8 @@
         return pltpu.make_async_remote_copy(
             src_ref=pooled.at[spot],
             dst_ref=pooled.at[spot],
-            send_sem=r["pool_s"].at[shift],
-            recv_sem=r["pool_r"].at[spot],
+            send_sem=r.pool_s.at[shift],
+            recv_sem=r.pool_r.at[spot],
             device_id={"dp": from_dp, "mp": from_mp},
             device_id_type=MESH,
         )
@@ -530,49 +588,49 @@
     for shift in range(1, members):
         pool_copy(shift).start()
 
-    def to_owner(source, kind, block):
+    def to_owner(source, target, sems, block):
         return pltpu.make_async_remote_copy(
             src_ref=source.at[block],
-            dst_ref=(normed_all if kind == "normed" else outer_all).at[dp_me, lax.rem(block, share)],
-            send_sem=r[kind + "_s"].at[block],
-            recv_sem=r[kind + "_r"].at[dp_me, lax.rem(block, share)],
+            dst_ref=target.at[dp_me, lax.rem(block, share)],
+            send_sem=sems[0].at[block],
+            recv_sem=sems[1].at[dp_me, lax.rem(block, share)],
             device_id={"dp": block // share},
             device_id_type=MESH,
         )
 
-    def from_member(target, kind, member, step):
+    def from_member(target, sems, member, step):
         return pltpu.make_async_remote_copy(
             src_ref=target.at[member, step],
             dst_ref=target.at[member, step],
-            send_sem=r[kind + "_s"].at[0],
-            recv_sem=r[kind + "_r"].at[member, step],
+            send_sem=sems[0].at[0],
+            recv_sem=sems[1].at[member, step],
             device_id={"dp": member},
             device_id_type=MESH,
         )
 
-    def whole_copy(target, kind, shift):
+    def whole_copy(target, sems, shift):
         return pltpu.make_async_remote_copy(
             src_ref=target.at[dp_me],
             dst_ref=target.at[dp_me],
-            send_sem=r[kind + "_s"].at[shift],
-            recv_sem=r[kind + "_r"].at[dp_me],
+            send_sem=sems[0].at[shift],
+            recv_sem=sems[1].at[dp_me],
             device_id={"dp": lax.rem(dp_me + shift, dp_count)},
             device_id_type=MESH,
         )
 
-    def whole_arrival(target, kind, shift):
+    def whole_arrival(target, sems, shift):
         member = lax.rem(dp_me + shift, dp_count)
         return pltpu.make_async_remote_copy(
             src_ref=target.at[member],
             dst_ref=target.at[member],
-            send_sem=r[kind + "_s"].at[shift],
-            recv_sem=r[kind + "_r"].at[member],
+            send_sem=sems[0].at[shift],
+            recv_sem=sems[1].at[member],
             device_id={"dp": member},
             device_id_type=MESH,
         )
 
     def normed_block(block, carry):
-        value = hidden[block].astype(F32) * r["inv_ref"][...] * gain_at(block)
+        value = hidden[block].astype(F32) * r.inv_ref[...] * gain_at(block)
         value = value.astype(BF16)
         mine = block // share == dp_me
 
@@ -582,14 +640,14 @@
 
         @pl.when(jnp.logical_not(mine))
         def _():
-            r["normed_out"][block] = value
-            to_owner(r["normed_out"], "normed", block).start()
+            r.normed_out[block] = value
+            to_owner(r.normed_out, normed_all, normed_sems, block).start()
 
         return carry
 
     lax.fori_loop(0, blocks, normed_block, 0)
     for shift in range(1, dp_count):
-        whole_copy(mixture_all, "mixture", shift).start()
+        whole_copy(mixture_all, mixture_sems, shift).start()
 
     for shift in range(1, members):
         pool_arrival(shift).wait_recv()
@@ -617,12 +675,12 @@
     for level in range(WIDTHS):
         packed = jnp.where(lane == level, losses[level], packed)
     losses_out[...] = packed[:, :WIDTHS]
-    slopes = r["slopes"]
+    slopes = r.slopes
     for p in range(pairs):
         slopes[2 * p] = query_slopes[p : p + 1]
         slopes[2 * p + 1] = passage_slopes[p : p + 1]
 
-    grad_in, mix_grad = r["grad_in"], r["mix_grad"]
+    grad_in, mix_grad = r.grad_in, r.mix_grad
     spot = lax.broadcasted_iota(jnp.int32, (length, 1), 0)
     shares = []
     for seq in range(seq_count):
@@ -649,8 +707,8 @@
 
         @pl.when(jnp.logical_not(mine))
         def _():
-            r["normed_out"][blocks + block] = outer
-            to_owner(r["normed_out"].at[pl.ds(blocks, blocks)], "outer", block).start()
+            outer_out[block] = outer
+            to_owner(outer_out, outer_all, outer_sems, block).start()
 
         mix_grad[...] += contract_last(outer, out_columns(block))
 
@@ -659,9 +717,9 @@
         stream_in(
             back,
             grad_in,
-            (r["relay_sb"], r["relay_rb"]),
-            (r["in_far_sb"], r["in_far_rb"]),
-            (r["in_near_sb"], r["in_near_rb"]),
+            (r.relay_sb, r.relay_rb),
+            (r.in_far_sb, r.in_far_rb),
+            (r.in_near_sb, r.in_near_rb),
             consume_back,
         )
 
@@ -681,14 +739,14 @@
         mixed = jnp.concatenate(
             [mix_grad[span, g * HEAD : (g + 1) * HEAD] for g in range(groups)], axis=0
         ).astype(BF16)
-        weights = r["prob_ref"][seq]
+        weights = r.prob_ref[seq]
         value_grad = contract_rows(weights.astype(BF16), mixed).astype(BF16)
-        pulled = contract_last(mixed, r["value_ref"][seq]).astype(BF16).astype(F32)
+        pulled = contract_last(mixed, r.value_ref[seq]).astype(BF16).astype(F32)
         score_grad = weights * (pulled - jnp.sum(weights * pulled, axis=1, keepdims=True))
         score_grad = (score_grad * HEAD ** (-0.5)).astype(BF16)
-        query_grad = jnp.dot(score_grad, r["key_ref"][seq], preferred_element_type=F32)
+        query_grad = jnp.dot(score_grad, r.key_ref[seq], preferred_element_type=F32)
         query_grad = query_grad.astype(BF16).astype(F32)
-        key_grad = contract_rows(score_grad, r["query_ref"][seq]).astype(BF16).astype(F32)
+        key_grad = contract_rows(score_grad, r.query_ref[seq]).astype(BF16).astype(F32)
         pieces = [
             rotary(query_grad[g * length : (g + 1) * length], table, -1.0).astype(BF16)
             for g in range(groups)
@@ -698,23 +756,23 @@
         head_grads[span, :] = joined
         row_dot.append(lane_sum(joined.astype(F32) * acc[span, :]))
     for shift in range(1, dp_count):
-        whole_copy(heads_all, "heads", shift).start()
+        whole_copy(heads_all, heads_sems, shift).start()
     row_dot = jnp.concatenate(row_dot, axis=0)
 
     def part_back(block):
         value = contract_last(head_grads[...], head_w[rows_at(block * width, width), :])
-        scaled = value * (hidden[block].astype(F32) * r["inv_ref"][...])
-        r["gain_part"][:, lanes_at(block * width, width)] = jnp.sum(scaled, axis=0, keepdims=True)
+        scaled = value * (hidden[block].astype(F32) * r.inv_ref[...])
+        r.gain_part[:, lanes_at(block * width, width)] = jnp.sum(scaled, axis=0, keepdims=True)
         return value
 
-    row_dots = r["row_dots"]
+    row_dots = r.row_dots
 
     def dots_copy(shift):
         return pltpu.make_async_remote_copy(
             src_ref=row_dots.at[mp_me],
             dst_ref=row_dots.at[mp_me],
-            send_sem=r["dots_s"].at[shift],
-            recv_sem=r["dots_r"].at[mp_me],
+            send_sem=r.dots_s.at[shift],
+            recv_sem=r.dots_r.at[mp_me],
             device_id={"mp": lax.rem(mp_me + shift, mp_count)},
             device_id_type=MESH,
         )
@@ -724,8 +782,8 @@
         return pltpu.make_async_remote_copy(
             src_ref=row_dots.at[member],
             dst_ref=row_dots.at[member],
-            send_sem=r["dots_s"].at[shift],
-            recv_sem=r["dots_r"].at[member],
+            send_sem=r.dots_s.at[shift],
+            recv_sem=r.dots_r.at[member],
             device_id={"mp": member},
             device_id_type=MESH,
         )
@@ -746,11 +804,11 @@
             for member in range(1, mp_count):
                 total = total + row_dots[member]
             column = lane_sum(jnp.where(diagonal, total, 0.0))
-            inverse = r["inv_ref"][...]
+            inverse = r.inv_ref[...]
             squares[:, :1] = column * inverse * inverse * inverse * (1.0 / width_all)
 
         def finish(block, total):
-            value = upstream(block) + total * gain_at(block) * r["inv_ref"][...]
+            value = upstream(block) + total * gain_at(block) * r.inv_ref[...]
             return (value - hidden[block].astype(F32) * squares[:, :1]).astype(BF16)
 
         stream_out(
@@ -759,16 +817,16 @@
             finish,
             grad_in,
             (
-                r["near_send_b"],
-                r["near_got_b"],
-                r["far_send_b"],
-                r["far_got_b"],
-                r["relay_send_b"],
+                r.near_send_b,
+                r.near_got_b,
+                r.far_send_b,
+                r.far_got_b,
+                r.relay_send_b,
                 prepare,
             ),
-            (r["relay_sb"], r["relay_rb"]),
-            (r["out_far_sb"], r["out_far_rb"]),
-            (r["out_near_sb"], r["out_near_rb"]),
+            (r.relay_sb, r.relay_rb),
+            (r.out_far_sb, r.out_far_rb),
+            (r.out_near_sb, r.out_near_rb),
         )
         for shift in range(1, mp_count):
             dots_copy(shift).wait_send()
@@ -781,16 +839,16 @@
 
         lax.fori_loop(0, blocks, body, 0)
 
-    gain_got = r["gain_got"]
+    gain_got = r.gain_got
     gain_cols = gain_got.shape[2]
 
     def gain_copy(shift):
         to_dp, to_mp, spot = peer(shift)
         return pltpu.make_async_remote_copy(
-            src_ref=r["gain_part"].at[:, lanes_at(spot * gain_cols, gain_cols)],
+            src_ref=r.gain_part.at[:, lanes_at(spot * gain_cols, gain_cols)],
             dst_ref=gain_got.at[me],
-            send_sem=r["gain_s"].at[shift],
-            recv_sem=r["gain_r"].at[me],
+            send_sem=r.gain_s.at[shift],
+            recv_sem=r.gain_r.at[me],
             device_id={"dp": to_dp, "mp": to_mp},
             device_id_type=MESH,
         )
@@ -800,15 +858,15 @@
         return pltpu.make_async_remote_copy(
             src_ref=gain_got.at[spot],
             dst_ref=gain_got.at[spot],
-            send_sem=r["gain_s"].at[shift],
-            recv_sem=r["gain_r"].at[spot],
+            send_sem=r.gain_s.at[shift],
+            recv_sem=r.gain_r.at[spot],
             device_id={"dp": from_dp, "mp": from_mp},
             device_id_type=MESH,
         )
 
     for shift in range(1, members):
         gain_copy(shift).start()
-    total = r["gain_part"][:, lanes_at(me * gain_cols, gain_cols)]
+    total = r.gain_part[:, lanes_at(me * gain_cols, gain_cols)]
     for shift in range(1, members):
         gain_arrival(shift).wait_recv()
         total = total + gain_got[lax.rem(me + shift, members)]
@@ -818,16 +876,16 @@
         pool_copy(shift).wait_send()
         gain_copy(shift).wait_send()
     for shift in range(1, dp_count):
-        whole_copy(mixture_all, "mixture", shift).wait_send()
-        whole_copy(heads_all, "heads", shift).wait_send()
-        whole_arrival(mixture_all, "mixture", shift).wait_recv()
-        whole_arrival(heads_all, "heads", shift).wait_recv()
+        whole_copy(mixture_all, mixture_sems, shift).wait_send()
+        whole_copy(heads_all, heads_sems, shift).wait_send()
+        whole_arrival(mixture_all, mixture_sems, shift).wait_recv()
+        whole_arrival(heads_all, heads_sems, shift).wait_recv()
 
     def drain(block, carry):
         @pl.when(block // share != dp_me)
         def _():
-            to_owner(r["normed_out"], "normed", block).wait_send()
-            to_owner(r["normed_out"].at[pl.ds(blocks, blocks)], "outer", block).wait_send()
+            to_owner(r.normed_out, normed_all, normed_sems, block).wait_send()
+            to_owner(outer_out, outer_all, outer_sems, block).wait_send()
 
         return carry
 
@@ -835,8 +893,8 @@
     for shift in range(1, dp_count):
         member = lax.rem(dp_me + shift, dp_count)
         for step in range(share):
-            from_member(normed_all, "normed", member, step).wait_recv()
-            from_member(outer_all, "outer", member, step).wait_recv()
+            from_member(normed_all, normed_sems, member, step).wait_recv()
+            from_member(outer_all, outer_sems, member, step).wait_recv()
 
 
 def step_pass(lengths, positives, entrance, gain, table, wq, wk, wv, wo):
@@ -867,13 +925,24 @@
         prob_ref=((seq_count, stacked, length), F32),
         pooled=((members, seq_count, width_all), F32),
         slopes=((dp_count * seq_count, 1, width_all), F32),
-        normed_out=((2 * blocks, *block), BF16),
+        normed_out=((blocks, *block), BF16),
+        outer_out=((blocks, *block), BF16),
         grad_in=((blocks, *block), BF16),
         mix_grad=((rows, query_cols), F32),
         row_dots=((mp_count, 1, row_pad), F32),
         gain_part=((1, width_all), F32),
         gain_got=((members, 1, width_all // members), F32),
         pool_ref=((pool_rows, rows), BF16),
+        near_send=((2 * SUB, *block), BF16),
+        near_got=((2 * SUB, *block), BF16),
+        far_send=((SUB, *block), BF16),
+        far_got=((SUB, *block), BF16),
+        relay_send=((SUB, *block), BF16),
+        near_send_b=((2 * SUB, *block), BF16),
+        near_got_b=((2 * SUB, *block), BF16),
+        far_send_b=((SUB, *block), BF16),
+        far_got_b=((SUB, *block), BF16),
+        relay_send_b=((SUB, *block), BF16),
     )
     counts = dict(
         load_sem=(4,),
@@ -892,17 +961,31 @@
         dots_r=(mp_count,),
         gain_s=(members,),
         gain_r=(members,),
-    )
-    for tail in ("", "_b"):
-        shapes["near_send" + tail] = shapes["near_got" + tail] = ((2 * SUB, *block), BF16)
-        shapes["far_send" + tail] = shapes["far_got" + tail] = ((SUB, *block), BF16)
-        shapes["relay_send" + tail] = ((SUB, *block), BF16)
-    for side in ("s", "r", "sb", "rb"):
-        counts["relay_" + side] = counts["in_far_" + side] = counts["out_far_" + side] = (SUB,)
-        counts["in_near_" + side] = counts["out_near_" + side] = (2 * SUB,)
-    scratch = [
-        pltpu.VMEM(*shapes[name]) if name in shapes else dma(counts[name]) for name in SCRATCH
-    ]
+        relay_s=(SUB,),
+        in_far_s=(SUB,),
+        out_far_s=(SUB,),
+        in_near_s=(2 * SUB,),
+        out_near_s=(2 * SUB,),
+        relay_r=(SUB,),
+        in_far_r=(SUB,),
+        out_far_r=(SUB,),
+        in_near_r=(2 * SUB,),
+        out_near_r=(2 * SUB,),
+        relay_sb=(SUB,),
+        in_far_sb=(SUB,),
+        out_far_sb=(SUB,),
+        in_near_sb=(2 * SUB,),
+        out_near_sb=(2 * SUB,),
+        relay_rb=(SUB,),
+        in_far_rb=(SUB,),
+        out_far_rb=(SUB,),
+        in_near_rb=(2 * SUB,),
+        out_near_rb=(2 * SUB,),
+    )
+    scratch = Scratch(
+        **{name: pltpu.VMEM(*shape) for name, shape in shapes.items()},
+        **{name: dma(count) for name, count in counts.items()},
+    )
     vmem = pl.BlockSpec(memory_space=pltpu.VMEM)
     smem = pl.BlockSpec(memory_space=pltpu.SMEM)
     hbm = pl.BlockSpec(memory_space=pltpu.HBM)
@@ -918,7 +1001,7 @@
         ),
         in_specs=[smem, smem, hbm, vmem, vmem, hbm, hbm, hbm, hbm],
         out_specs=(vmem,) * 6,
-        scratch_shapes=[pltpu.VMEM((blocks, *block), BF16)] + scratch,
+        scratch_shapes=[pltpu.VMEM((blocks, *block), BF16)] + list(scratch),
         compiler_params=pltpu.CompilerParams(
             collective_id=0, has_side_effects=True, vmem_limit_bytes=56 * 1024 * 1024
         ),

time: 220 us -> 220 us (level)
  no operation moved by 1% of the time
where the time goes in v1:
time: 220 us; the launch traced here: 219 us
  Pallas kernels  203 us (92%)
  matrix products  9.82 us (4%)
  local copies, waits for them, and re-layouts  5.82 us (3%)
    pallas_call x1, Pallas kernels, step_pass(): pl.pallas_call(step_kernel, out_shape=(jax.ShapeDtypeStruct((1, WIDTHS),...  203 us
    dot_general x4, matrix products, contract_rows(): lax.dot_general(left, right, (((0,), (0,)), ((), ())), preferred_element_...  9.82 us

profile of v1, /device:TPU:0, one launch (start us, length us, event | category | flops | bytes accessed | tf_op | source)
XLA Modules:
  0.0 219.5 jit_solution(15534006417942252897)
XLA Ops:
  0.6 203.2 %step_pass.1 = (f32[1,7]{1,0:T(1,128)}, f32[1,512]{1,0:T(1,128)}, bf16[2,8,192,256]{3,2,1,0:T(8,128)(2,1)}, bf16[2,192,512]{2,1,0:T(8,128)(2,1)}, bf16[2,8,192,2...) custom-call(s32[1,2]{1,0:T(1,128)} %lengths.1, s32[2]{0:T(128)} %positives.1, bf16[192,4096]{1,0:T(8,128)(2,1)} %bitcast.36, ...), custom_call_target="tpu_custom_call" | custom-call | tf_op jit(solution)/shard_map/step_pass/pallas_call | solution.py:992
  203.8 2.3 %copy.15 = bf16[2,192,8,256]{3,2,1,0:T(8,128)(2,1)S(1)} copy(bf16[2,192,8,256]{3,1,2,0:T(8,128)(2,1)} %bitcast.38) | data formatting | bytes 3145728 | tf_op jit(solution)/shard_map/transpose | solution.py:1028
  206.1 0.0 copy-start.1
  206.1 0.5 copy.17
  206.6 0.6 copy-done.1
  207.1 1.6 convolution_bitcast_fusion.2
  208.7 0.0 copy-start
  208.8 1.6 convolution_bitcast_fusion.3
  210.3 0.0 copy-done
  210.3 0.9 copy.16
  211.2 0.5 copy.18
  211.7 0.0 copy-start.2
  211.7 3.3 %convolution_bitcast_fusion.1 = f32[1,2048,512]{2,1,0:T(8,128)} fusion(bf16[384,2048]{1,0:T(8,128)(2,1)S(1)} %bitcast.30, bf16[384,768]{1,0:T(8,128)(2,1)S(1)} %bitcast.43), kind=kOutput, calls=%fused_computation.1 | convolution fusion | flops 805306368 | bytes 6160384 | tf_op jit(solution)/shard_map/dot_general | solution.py:26
  215.1 0.0 copy-done.2
  215.1 0.0 copy-start.4
  215.1 0.0 copy-start.3
  215.1 3.3 %convolution_bitcast_fusion = f32[1,512,2048]{2,1,0:T(8,128)} fusion(bf16[384,512]{1,0:T(8,128)(2,1)S(1)} %bitcast.44, bf16[384,2048]{1,0:T(8,128)(2,1)S(1)} %bitcast.33), kind=kOutput, calls=%fused_computation | convolution fusion | flops 805306368 | bytes 6160384 | tf_op jit(solution)/shard_map/dot_general | solution.py:26
  218.4 0.0 copy-done.4
  218.4 0.5 copy.21
  218.9 0.0 copy-done.3
  218.9 0.6 copy.22
Async XLA Ops:
  206.1 1.1 copy-start.1
  208.7 1.6 copy-start
  211.7 3.3 %copy-start.2 = (bf16[2,192,512]{2,1,0:T(8,128)(2,1)S(1)}, bf16[2,192,512]{2,1,0:T(8,128)(2,1)}, u32[]{:S(2)}) copy-start(bf16[2,192,512]{2,1,0:T(8,128)(2,1)} %get-tuple-element.16) | copy-start | bytes 1179652
  215.1 3.3 %copy-start.4 = (f32[1,7]{1,0:T(1,128)S(1)}, f32[1,7]{1,0:T(1,128)}, u32[]{:S(2)}) copy-start(f32[1,7]{1,0:T(1,128)} %get-tuple-element.24) | copy-start | bytes 88
  215.1 3.8 %copy-start.3 = (f32[1,512]{1,0:T(1,128)S(1)}, f32[1,512]{1,0:T(1,128)}, u32[]{:S(2)}) copy-start(f32[1,512]{1,0:T(1,128)} %get-tuple-element.25) | copy-start | bytes 6148

commit v2 on v1

--- a/solution.py
+++ b/solution.py
@@ -451,7 +451,6 @@
     expected = (
         members - 1 + forth.has_source.astype(jnp.int32) + forth.has_target.astype(jnp.int32)
     )
-    pl.semaphore_wait(barrier, expected)
 
     def gain_at(block):
         return gain[:, lanes_at(block * width, width)]
@@ -470,6 +469,7 @@
 
     @pl.when(forth.has_source)
     def _():
+        pl.semaphore_wait(barrier, expected)
         stream_in(
             forth,
             hidden,
@@ -486,7 +486,8 @@
             consume(block)
             return carry
 
-        lax.fori_loop(0, blocks, body, 0)
+        lax.fori_loop(0, blocks, body, 0, unroll=4)
+        pl.semaphore_wait(barrier, expected)
 
     inv_rms = lax.rsqrt(
         jnp.sum(squares[...], axis=1, keepdims=True) * (1.0 / width_all) + EPSILON
@@ -1009,6 +1010,58 @@
     )(lengths, positives, entrance, gain, table, wq, wk, wv, wo)
 
 
+def weight_kernel(
+    normed, mixture, outer, heads, query_grad, key_grad, value_grad, out_grad, turned
+):
+    members, rows = heads.shape[:2]
+    query_cols, kv_cols = query_grad.shape[1], key_grad.shape[1]
+
+    @pl.when(pl.program_id(0) == 0)
+    def _():
+        for member in range(members):
+            turned[:, member * rows : (member + 1) * rows] = mixture[member].T
+
+    inputs = jnp.concatenate([normed[member, 0] for member in range(members)], axis=0)
+    grads = jnp.concatenate([heads[member] for member in range(members)], axis=0)
+    product = contract_rows(inputs, grads)
+    query_grad[...] = product[:, :query_cols]
+    key_grad[...] = product[:, query_cols : query_cols + kv_cols]
+    value_grad[...] = product[:, query_cols + kv_cols :]
+    grads = jnp.concatenate([outer[member, 0] for member in range(members)], axis=0)
+    out_grad[...] = jnp.dot(turned[...], grads, preferred_element_type=F32)
+
+
+def weight_grads(normed, mixture, outer, heads, query_cols, kv_cols):
+    members, share, rows, width = normed.shape
+    columns = share * width
+    streamed = pl.BlockSpec((members, 1, rows, width), lambda step: (0, step, 0, 0))
+    vmem = pl.BlockSpec(memory_space=pltpu.VMEM)
+
+    def tall(cols):
+        return pl.BlockSpec((width, cols), lambda step: (step, 0))
+
+    return pl.pallas_call(
+        weight_kernel,
+        grid=(share,),
+        in_specs=[streamed, vmem, streamed, vmem],
+        out_specs=(
+            tall(query_cols),
+            tall(kv_cols),
+            tall(kv_cols),
+            pl.BlockSpec((query_cols, width), lambda step: (0, step)),
+        ),
+        out_shape=(
+            jax.ShapeDtypeStruct((columns, query_cols), F32),
+            jax.ShapeDtypeStruct((columns, kv_cols), F32),
+            jax.ShapeDtypeStruct((columns, kv_cols), F32),
+            jax.ShapeDtypeStruct((query_cols, columns), F32),
+        ),
+        scratch_shapes=[pltpu.VMEM((query_cols, members * rows), BF16)],
+        compiler_params=pltpu.CompilerParams(dimension_semantics=("arbitrary",)),
+        name="weight_grads",
+    )(normed, mixture, outer, heads)
+
+
 def local(entrance, lengths, positives, norm_gains, query_proj, key_proj, value_proj, out_proj):
     length = entrance.shape[2]
     width_all = entrance.shape[3]
@@ -1025,17 +1078,16 @@
         value_proj[0],
         out_proj[0],
     )
-    normed = normed.transpose(0, 2, 1, 3).reshape(heads.shape[0] * heads.shape[1], -1)
-    outer = outer.transpose(0, 2, 1, 3).reshape(heads.shape[0] * heads.shape[1], -1)
-    heads = heads.reshape(normed.shape[0], -1)
-    mixture = mixture.reshape(normed.shape[0], -1)
+    query_grad, key_grad, value_grad, out_grad = weight_grads(
+        normed, mixture, outer, heads, query_cols, kv_cols
+    )
     return (
         losses,
         gain_share,
-        contract_rows(normed, heads[:, :query_cols])[None],
-        contract_rows(normed, heads[:, query_cols : query_cols + kv_cols])[None],
-        contract_rows(normed, heads[:, query_cols + kv_cols :])[None],
-        contract_rows(mixture, outer)[None],
+        query_grad[None],
+        key_grad[None],
+        value_grad[None],
+        out_grad[None],
     )
 
 

time: 220 us -> 216 us (0.982)
  matrix products: 9.82 us -> 0 us
  Pallas kernels: 203 us -> 212 us
  local copies, waits for them, and re-layouts: 5.82 us -> 2.35 us
    pallas_call x0 -> x1, Pallas kernels: none -> 9.9 us  [weight_grads(): pl.pallas_call(weight_kernel, grid=(share,), in_specs=[streamed, vmem, st...]
    dot_general x4 -> x0, matrix products: 9.82 us -> none  [contract_rows(): lax.dot_general(left, right, (((0,), (0,)), ((), ())), preferred_element_...]
    transpose x2 -> x0, local copies, waits for them, and re-layouts: 3.18 us -> none  [the longest x1 2.29 us: local(): normed.transpose(0, 2, 1, 3).reshape(heads.shape[0] * heads.shape[1], -1)]
where the time goes in v2:
time: 216 us; the launch traced here: 215 us
  Pallas kernels  212 us (98%)
  local copies, waits for them, and re-layouts  2.35 us (1%)
    pallas_call x1, Pallas kernels, step_pass(): pl.pallas_call(step_kernel, out_shape=(jax.ShapeDtypeStruct((1, WIDTHS),...  203 us
    pallas_call x1, Pallas kernels, weight_grads(): pl.pallas_call(weight_kernel, grid=(share,), in_specs=[streamed, vmem, st...  9.9 us

profile of v2, /device:TPU:0, one launch (start us, length us, event | category | flops | bytes accessed | tf_op | source)
XLA Modules:
  0.0 215.5 jit_solution(7572235365540357308)
XLA Ops:
  0.6 202.6 %step_pass.1 = (f32[1,7]{1,0:T(1,128)}, f32[1,512]{1,0:T(1,128)}, bf16[2,8,192,256]{3,2,1,0:T(8,128)(2,1)}, bf16[2,192,512]{2,1,0:T(8,128)(2,1)}, bf16[2,8,192,2...) custom-call(s32[1,2]{1,0:T(1,128)} %lengths.1, s32[2]{0:T(128)} %positives.1, bf16[192,4096]{1,0:T(8,128)(2,1)} %bitcast.11, ...), custom_call_target="tpu_custom_call" | custom-call | tf_op jit(solution)/shard_map/step_pass/pallas_call | solution.py:993
  203.2 9.9 %weight_grads.1 = (f32[2048,512]{1,0:T(8,128)}, f32[2048,128]{1,0:T(8,128)}, f32[2048,128]{1,0:T(8,128)}, f32[512,2048]{1,0:T(8,128)}) custom-call(bf16[2,8,192,256]{3,2,1,0:T(8,128)(2,1)} %get-tuple-element.18.normed, bf16[2,192,512]{2,1,0:T(8,128)(2,1)} %get-tuple-element.19.mixture, bf16[2,8,192,256]{3,2,1,0:T(8,128)(2,1)} %get-tuple-element.20.outer, ...), custom_call_target="tpu_custom_call" | custom-call | tf_op jit(solution)/shard_map/weight_grads/pallas_call | solution.py:1043
  213.1 1.1 copy.17
  214.2 1.2 copy.18

commit v3 on v2

v3 whole, which is shorter than its diff:
```python
from typing import NamedTuple

import jax
import jax.numpy as jnp
import numpy as np
from jax import lax
from jax.experimental import pallas as pl
from jax.experimental.pallas import tpu as pltpu
from jax.sharding import PartitionSpec as P

HEAD = 128
WIDTHS = 7


EPSILON = 1e-05
SOFTMAX_TEMPER = 0.05
ROPE_BASE = 500000.0
MESH = pl.DeviceIdType.MESH
ROW_TILE = 16
SUB = 4
RELAY, CROSS, TAKE, ATTEND, NEAR, FAR, NEAR_OWN, OWN, FINISH = range(9)
FORWARD_ORDER = (
    (RELAY, 0, 0, 1, 2, 3), (CROSS, 0, 0, 2, 1), (TAKE, 0, 0), (RELAY, 1, 0), (CROSS, 0, 3),
    (TAKE, 0, 2), (RELAY, 1, 1), (TAKE, 0, 1, 3), (RELAY, 1, 2), (ATTEND, 0, 0), (NEAR, 0, 0, 1),
    (RELAY, 1, 3), (NEAR_OWN, 0, 2, 0), (NEAR, 0, 2), (CROSS, 1, 0), (NEAR, 0, 3), (FAR, 0, 0),
    (NEAR_OWN, 0, 1), (FAR, 0, 1), (OWN, 0, 0), (CROSS, 1, 1), (TAKE, 1, 0), (CROSS, 1, 2),
    (FAR, 0, 2, 3), (OWN, 0, 1), (CROSS, 1, 3), (TAKE, 1, 1, 2), (FINISH, 0, 0), (TAKE, 1, 3),
    (ATTEND, 1, 0), (FINISH, 0, 1), (NEAR, 1, 0), (NEAR_OWN, 0, 3), (OWN, 0, 2), (NEAR, 1, 1),
    (FINISH, 0, 2), (NEAR_OWN, 1, 0), (FAR, 1, 0), (OWN, 0, 3), (FINISH, 0, 3), (NEAR, 1, 2, 3),
    (FAR, 1, 1), (NEAR_OWN, 1, 2), (FAR, 1, 2), (NEAR_OWN, 1, 1), (FAR, 1, 3), (OWN, 1, 0),
    (FINISH, 1, 0), (NEAR_OWN, 1, 3), (OWN, 1, 1), (FINISH, 1, 1), (OWN, 1, 2, 3),
    (FINISH, 1, 2, 3),
)
BACKWARD_ORDER = (
    (RELAY, 0, 0, 1, 2, 3), (CROSS, 0, 0, 1), (TAKE, 0, 0), (CROSS, 0, 2), (TAKE, 0, 1),
    (CROSS, 0, 3), (TAKE, 0, 2, 3), (ATTEND, 0, 0), (NEAR, 0, 0), (NEAR_OWN, 0, 0),
    (NEAR, 0, 1, 2), (FAR, 0, 0), (NEAR, 0, 3), (FAR, 0, 1, 2), (NEAR_OWN, 0, 2, 1), (OWN, 0, 0),
    (FAR, 0, 3), (FINISH, 0, 0), (RELAY, 1, 0), (OWN, 0, 2, 1), (RELAY, 1, 1), (FINISH, 0, 1),
    (NEAR_OWN, 0, 3), (RELAY, 1, 2), (FINISH, 0, 2), (OWN, 0, 3), (RELAY, 1, 3), (FINISH, 0, 3),
    (CROSS, 1, 0, 1), (TAKE, 1, 0), (CROSS, 1, 2), (TAKE, 1, 1), (CROSS, 1, 3), (TAKE, 1, 2, 3),
    (ATTEND, 1, 0), (NEAR, 1, 0, 1), (NEAR_OWN, 1, 0), (NEAR, 1, 3), (FAR, 1, 0), (NEAR, 1, 2),
    (FAR, 1, 1), (OWN, 1, 0), (NEAR_OWN, 1, 1), (FAR, 1, 2, 3), (NEAR_OWN, 1, 2), (FINISH, 1, 0),
    (OWN, 1, 1), (NEAR_OWN, 1, 3), (FINISH, 1, 1), (OWN, 1, 2), (FINISH, 1, 2), (OWN, 1, 3),
    (FINISH, 1, 3),
)
F32 = jnp.float32
BF16 = jnp.bfloat16


def contract_rows(left, right):
    return lax.dot_general(
        left, right, (((0,), (0,)), ((), ())), preferred_element_type=jnp.float32
    )


def contract_last(left, right):
    return lax.dot_general(
        left, right, (((left.ndim - 1,), (1,)), ((), ())), preferred_element_type=jnp.float32
    )


def rotary_constants(length):
    half_size = HEAD // 2
    frequencies = ROPE_BASE ** (-np.arange(half_size, dtype=np.float64) * 2.0 / HEAD)
    angles = np.arange(length, dtype=np.float64)[:, None] * frequencies[None, :]
    cosine = np.concatenate([np.cos(angles), np.cos(angles)], axis=1)
    sine = np.concatenate([-np.sin(angles), np.sin(angles)], axis=1)
    return np.stack([cosine, sine]).astype(np.float32)


def mp_place(me, levels):
    bits = [(me // (1 << level)) % 2 for level in range(levels)]
    partners = [me + (1 - 2 * bits[level]) * (1 << level) for level in range(levels)]
    return bits, partners


def rows_at(start, size):
    return pl.ds(pl.multiple_of(start, ROW_TILE), size)


def lanes_at(start, size):
    return pl.ds(pl.multiple_of(start, 128), size)


class Place:
    def __init__(self, direction):
        self.here = lax.axis_index("section")
        self.count = lax.axis_size("section")
        (self.low, self.high), (self.near, self.far) = mp_place(lax.axis_index("mp"), 2)
        self.direction = direction
        if direction > 0:
            self.has_source, self.has_target = self.here > 0, self.here < self.count - 1
        else:
            self.has_source, self.has_target = self.here < self.count - 1, self.here > 0

    def quarter(self, flip_low, flip_high):
        low = 1 - self.low if flip_low else self.low
        high = 1 - self.high if flip_high else self.high
        return (low * 2 + high) * SUB


def send(source, target, sems, slot, **device):
    return pltpu.make_async_remote_copy(
        src_ref=source,
        dst_ref=target,
        send_sem=sems[0].at[slot],
        recv_sem=sems[1].at[slot],
        device_id=device,
        device_id_type=MESH,
    )


class StreamIn:
    def __init__(self, place, group, buf, relay, far, near):
        self.place, self.buf = place, buf
        self.relay, self.far, self.near = relay, far, near
        self.group = group

    def at(self, block):
        return self.buf.at[self.group * 4 * SUB + block]

    def relay_copy(self, step, block):
        slot = self.group * SUB + step
        return send(self.at(block), self.at(block), self.relay, slot, section=self.place.here)

    def near_copy(self, slot, block):
        slot = self.group * 2 * SUB + slot
        return send(self.at(block), self.at(block), self.near, slot, mp=self.place.near)

    def far_copy(self, step, block):
        slot = self.group * SUB + step
        return send(self.at(block), self.at(block), self.far, slot, mp=self.place.far)

    def relay_step(self, step):
        block = self.place.quarter(0, 0) + step
        self.relay_copy(step, block).wait_recv()
        self.far_copy(step, block).start()
        self.near_copy(step, block).start()

    def cross_step(self, step):
        block = self.place.quarter(0, 1) + step
        self.far_copy(step, block).wait_recv()
        self.near_copy(SUB + step, block).start()

    def settle(self, step):
        self.near_copy(step, self.place.quarter(1, 0) + step).wait_recv()
        self.near_copy(SUB + step, self.place.quarter(1, 1) + step).wait_recv()

    def drain(self):
        own, other = self.place.quarter(0, 0), self.place.quarter(0, 1)
        for step in range(SUB):
            self.far_copy(step, own + step).wait_send()
            self.near_copy(step, own + step).wait_send()
            self.near_copy(SUB + step, other + step).wait_send()


class StreamOut:
    def __init__(self, place, group, part, finish, dest, bufs, relay, far, near):
        self.place, self.group = place, group
        self.part_of, self.finish_of, self.dest = part, finish, dest
        self.near_send, self.near_got, self.far_send, self.far_got, self.relay_send, self.keep = (
            bufs
        )
        self.relay_sems, self.far_sems, self.near_sems = relay, far, near

    def near_copy(self, slot):
        slot = self.group * 2 * SUB + slot
        return send(
            self.near_send.at[slot], self.near_got.at[slot], self.near_sems, slot, mp=self.place.near
        )

    def far_copy(self, step):
        slot = self.group * SUB + step
        return send(
            self.far_send.at[slot], self.far_got.at[slot], self.far_sems, slot, mp=self.place.far
        )

    def relay_copy(self, step):
        slot = self.group * SUB + step
        place = self.place
        return send(
            self.relay_send.at[slot],
            self.dest.at[self.group * 4 * SUB + place.quarter(0, 0) + step],
            self.relay_sems,
            slot,
            section=place.here + place.direction,
        )

    def near(self, flip, step):
        place = self.place
        slot = (1 - place.high if flip else place.high) * SUB + step
        value = self.part_of(self.group, place.quarter(1, flip) + step)
        self.near_send[self.group * 2 * SUB + slot] = value.astype(BF16)
        self.near_copy(slot).start()

    def arrived(self, slot):
        self.near_copy(slot).wait_recv()
        return self.near_got[self.group * 2 * SUB + slot].astype(F32)

    def far(self, step):
        place = self.place
        value = self.part_of(self.group, place.quarter(0, 1) + step)
        value = value + self.arrived((1 - place.high) * SUB + step)
        self.far_send[self.group * SUB + step] = value.astype(BF16)
        self.far_copy(step).start()

    def own(self, step):
        place = self.place
        value = self.part_of(self.group, place.quarter(0, 0) + step)
        self.keep[self.group * SUB + step] = value + self.arrived(place.high * SUB + step)

    def finish(self, step):
        slot = self.group * SUB + step
        block = self.place.quarter(0, 0) + step
        self.far_copy(step).wait_recv()
        value = self.keep[slot] + self.far_got[slot].astype(F32)
        self.relay_send[slot] = self.finish_of(self.group, block, value)
        self.relay_copy(step).start()

    def drain(self):
        for step in range(SUB):
            self.far_copy(step).wait_send()
            self.relay_copy(step).wait_send()
        for slot in range(2 * SUB):
            self.near_copy(slot).wait_send()


def run_pass(order, ins, outs, has_source, has_target, consume, attend, prepare, rest):
    def take(group, step):
        @pl.when(has_source)
        def _():
            ins[group].settle(step)

        for quarter in range(4):
            consume(group, quarter * SUB + step)

    def finish(group, step):
        if step == 0:
            prepare(group)
        outs[group].finish(step)

    receive = {
        RELAY: lambda group, step: ins[group].relay_step(step),
        CROSS: lambda group, step: ins[group].cross_step(step),
    }
    produce = {
        NEAR: lambda group, step: outs[group].near(1, step),
        NEAR_OWN: lambda group, step: outs[group].near(0, step),
        FAR: lambda group, step: outs[group].far(step),
        OWN: lambda group, step: outs[group].own(step),
        FINISH: finish,
    }
    for kind, group, *steps in order:
        if kind == ATTEND:
            attend(group)
            if rest is not None:
                pl.when(jnp.logical_not(has_target))(lambda group=group: rest(group))
        elif kind == TAKE:
            for step in steps:
                take(group, step)
        else:
            action = receive.get(kind) or produce[kind]

            @pl.when(has_source if kind in receive else has_target)
            def _(group=group, steps=steps, action=action):
                for step in steps:
                    action(group, step)


def drain_pass(ins, outs, has_source, has_target):
    @pl.when(has_source)
    def _():
        for flow in ins:
            flow.drain()

    @pl.when(has_target)
    def _():
        for flow in outs:
            flow.drain()


def rotary(values, table, sign):
    turned = pltpu.roll(values, HEAD // 2, axis=1)
    return values * table[0] + turned * (table[1] * sign)


def fold_lanes(values):
    total = values[:, :128]
    for lane in range(1, values.shape[1] // 128):
        total = total + values[:, lane * 128 : (lane + 1) * 128]
    return total


def lane_sum(values):
    return jnp.sum(fold_lanes(values), axis=1, keepdims=True)


def matryoshka(queries, passages, target):
    pairs, width_all = queries.shape
    widths = [width_all >> level for level in range(WIDTHS)]
    bounds = [0] + widths[::-1]
    lane = lax.broadcasted_iota(jnp.int32, (pairs, 128), 1)

    def segment_sums(product):
        sums = []
        for low, high in zip(bounds[:-1], bounds[1:]):
            if high <= 128:
                inside = jnp.logical_and(lane >= low, lane < high)
                piece = jnp.where(inside, product[:, :128], 0.0)
            else:
                piece = fold_lanes(product[:, low:high])
            sums.append(jnp.sum(piece, axis=1, keepdims=True))
        for index in range(1, len(sums)):
            sums[index] = sums[index] + sums[index - 1]
        return sums[::-1]

    query_squares = segment_sums(queries * queries)
    passage_squares = segment_sums(passages * passages)
    dots = [segment_sums(queries * passages[j : j + 1]) for j in range(pairs)]
    losses = []
    mixed = [[] for _ in range(pairs)]
    query_own, passage_own = [], []
    for level, width in enumerate(widths):
        query_inv = lax.rsqrt(query_squares[level] * (1.0 / width) + 1e-06)
        passage_inv = lax.rsqrt(passage_squares[level] * (1.0 / width) + 1e-06)
        factors = [
            query_inv * passage_inv[j : j + 1] * (1.0 / (width * SOFTMAX_TEMPER))
            for j in range(pairs)
        ]
        logits = [dots[j][level] * factors[j] for j in range(pairs)]
        highest = logits[0]
        for j in range(1, pairs):
            highest = jnp.maximum(highest, logits[j])
        powers = [jnp.exp(logits[j] - highest) for j in range(pairs)]
        total = powers[0]
        picked = logits[0] * target[:, 0:1]
        for j in range(1, pairs):
            total = total + powers[j]
            picked = picked + logits[j] * target[:, j : j + 1]
        gap = jnp.log(total) + highest - picked
        losses.append(jnp.sum(gap, axis=0, keepdims=True) * (1.0 / pairs))
        slopes = [
            (powers[j] / total - target[:, j : j + 1]) * (1.0 / pairs) for j in range(pairs)
        ]
        pulls = [slopes[j] * logits[j] for j in range(pairs)]
        row_pull = pulls[0]
        for j in range(1, pairs):
            row_pull = row_pull + pulls[j]
        column_pull = jnp.concatenate(
            [jnp.sum(pulls[j], axis=0, keepdims=True) for j in range(pairs)], axis=0
        )
        for j in range(pairs):
            mixed[j].append(slopes[j] * factors[j])
        query_own.append(row_pull * query_inv * query_inv * (-1.0 / width))
        passage_own.append(column_pull * passage_inv * passage_inv * (-1.0 / width))
    for series in mixed + [query_own, passage_own]:
        for level in range(1, WIDTHS):
            series[level] = series[level] + series[level - 1]
    turned = [
        [
            jnp.concatenate([mixed[j][level][p : p + 1] for j in range(pairs)], axis=0)
            for level in range(WIDTHS)
        ]
        for p in range(pairs)
    ]

    def spread(own, own_rows, weights, rows):
        pieces = []
        low = 0
        while low < width_all:
            inside = [k for k in range(WIDTHS) if low < bounds[k + 1] and low + 128 > bounds[k]]
            high = max(low + 128, bounds[inside[-1] + 1])

            def coefficient(series, inside=inside):
                value = series[WIDTHS - 1 - inside[-1]]
                for k in reversed(inside[:-1]):
                    value = jnp.where(lane < bounds[k + 1], series[WIDTHS - 1 - k], value)
                return value

            def columns(values, low=low, high=high):
                return values[:, low:high]

            piece = coefficient(own) * columns(own_rows)
            for j in range(pairs):
                piece = piece + coefficient(weights[j]) * columns(rows[j : j + 1])
            pieces.append(piece)
            low = high
        return jnp.concatenate(pieces, axis=1)

    return (
        losses,
        spread(query_own, queries, mixed, passages),
        spread(passage_own, passages, turned, queries),
    )


class Scratch(NamedTuple):
    head_w: object
    out_w: object
    acc: object
    squares: object
    inv_ref: object
    query_ref: object
    key_ref: object
    value_ref: object
    prob_ref: object
    pooled: object
    slopes: object
    normed_out: object
    outer_out: object
    grad_in: object
    mix_grad: object
    row_dots: object
    gain_part: object
    hidden_sum: object
    pull_ref: object
    keep: object
    keep_b: object
    gain_got: object
    pool_ref: object
    near_send: object
    near_got: object
    far_send: object
    far_got: object
    relay_send: object
    near_send_b: object
    near_got_b: object
    far_send_b: object
    far_got_b: object
    relay_send_b: object
    load_sem: object
    enter_sem: object
    relay_s: object
    relay_r: object
    in_far_s: object
    in_far_r: object
    in_near_s: object
    in_near_r: object
    out_far_s: object
    out_far_r: object
    out_near_s: object
    out_near_r: object
    relay_sb: object
    relay_rb: object
    in_far_sb: object
    in_far_rb: object
    in_near_sb: object
    in_near_rb: object
    out_far_sb: object
    out_far_rb: object
    out_near_sb: object
    out_near_rb: object
    pool_s: object
    pool_r: object
    normed_s: object
    normed_r: object
    mixture_s: object
    mixture_r: object
    outer_s: object
    outer_r: object
    heads_s: object
    heads_r: object
    dots_s: object
    dots_r: object
    gain_s: object
    gain_r: object


def step_kernel(
    lengths,
    positives,
    entrance,
    gain,
    table,
    wq,
    wk,
    wv,
    wo,
    losses_out,
    gain_out,
    normed_all,
    mixture_all,
    outer_all,
    heads_all,
    hidden,
    *scratch,
):
    r = Scratch(*scratch)
    head_w, out_w, acc, squares = r.head_w, r.out_w, r.acc, r.squares
    forth, back = Place(1), Place(-1)
    rows, width = hidden.shape[1:]
    blocks = hidden.shape[0] // 2
    width_all = blocks * width
    pair_count = lengths.shape[0]
    seq_count = 2 * pair_count
    length = rows // pair_count
    query_cols, kv_cols = wq.shape[1], wk.shape[1]
    groups = query_cols // HEAD
    dp_me, mp_me = lax.axis_index("dp"), lax.axis_index("mp")
    dp_count, mp_count = lax.axis_size("dp"), lax.axis_size("mp")
    members = dp_count * mp_count
    me = dp_me * mp_count + mp_me
    share = blocks // dp_count
    row_pad = r.row_dots.shape[2]
    normed_sems, outer_sems = (r.normed_s, r.normed_r), (r.outer_s, r.outer_r)
    mixture_sems, heads_sems = (r.mixture_s, r.mixture_r), (r.heads_s, r.heads_r)
    outer_out = r.outer_out

    def peer(shift):
        spot = lax.rem(me + shift, members)
        return spot // mp_count, lax.rem(spot, mp_count), spot

    def span_of(group):
        return slice(group * rows, (group + 1) * rows)

    def sequences(group):
        for local_seq in range(pair_count):
            inner = slice(local_seq * length, (local_seq + 1) * length)
            outer = slice(group * rows + inner.start, group * rows + inner.stop)
            yield group * pair_count + local_seq, inner, outer

    def count_of(seq):
        return lengths[seq // 2, seq % 2]

    spot = lax.broadcasted_iota(jnp.int32, (length, 1), 0)

    def valid_of(seq):
        return jnp.where(spot < count_of(seq), 1.0, 0.0)

    loads = [
        pltpu.make_async_copy(wq, head_w.at[:, :query_cols], r.load_sem.at[0]),
        pltpu.make_async_copy(wk, head_w.at[:, query_cols : query_cols + kv_cols], r.load_sem.at[1]),
        pltpu.make_async_copy(wv, head_w.at[:, query_cols + kv_cols :], r.load_sem.at[2]),
        pltpu.make_async_copy(wo, out_w, r.load_sem.at[3]),
    ]

    def enter(group, block):
        slot = group * blocks + block
        return pltpu.make_async_copy(
            entrance.at[pl.ds(group * rows, rows), lanes_at(block * width, width)],
            hidden.at[slot],
            r.enter_sem.at[slot],
        )

    @pl.when(jnp.logical_not(forth.has_source))
    def _():
        for group in range(2):
            for block in range(blocks):
                enter(group, block).start()

    for load in loads:
        load.start()
    barrier = pltpu.get_barrier_semaphore()
    for shift in range(1, members):
        to_dp, to_mp, _ = peer(shift)
        pl.semaphore_signal(
            barrier, inc=1, device_id={"dp": to_dp, "mp": to_mp}, device_id_type=MESH
        )

    @pl.when(forth.has_source)
    def _():
        pl.semaphore_signal(
            barrier, inc=1, device_id={"section": forth.here - 1}, device_id_type=MESH
        )

    @pl.when(forth.has_target)
    def _():
        pl.semaphore_signal(
            barrier, inc=1, device_id={"section": forth.here + 1}, device_id_type=MESH
        )

    acc[...] = jnp.zeros_like(acc)
    squares[...] = jnp.zeros_like(squares)
    r.mix_grad[...] = jnp.zeros_like(r.mix_grad)
    r.gain_part[...] = jnp.zeros_like(r.gain_part)

    @pl.when(jnp.logical_not(back.has_source))
    def _():
        def clear(block, carry):
            r.grad_in[block] = jnp.zeros((rows, width), BF16)
            return carry

        lax.fori_loop(0, 2 * blocks, clear, 0)

    pool_shape = r.pool_ref.shape
    column = lax.broadcasted_iota(jnp.int32, pool_shape, 1)
    line = lax.broadcasted_iota(jnp.int32, pool_shape, 0)
    picks = jnp.zeros(pool_shape, F32)
    for seq in range(seq_count):
        inside = jnp.logical_and(column >= seq * length, column < seq * length + count_of(seq))
        picks = jnp.where(jnp.logical_and(line == seq, inside), 1.0, picks)
    r.pool_ref[...] = picks.astype(BF16)
    for load in loads[:3]:
        load.wait()
    expected = (
        members - 1 + forth.has_source.astype(jnp.int32) + forth.has_target.astype(jnp.int32)
    )

    @pl.when(forth.has_source)
    def _():
        pl.semaphore_wait(barrier, expected)

    def gain_at(block):
        return gain[:, lanes_at(block * width, width)]

    def out_columns(block):
        return out_w[:, lanes_at(block * width, width)]

    def consume(group, block):
        slot = group * blocks + block

        @pl.when(jnp.logical_not(forth.has_source))
        def _():
            enter(group, block).wait()

        value = hidden[slot].astype(F32)
        span = span_of(group)
        squares[span, :] += fold_lanes(value * value)
        for seq, inner, _ in sequences(group):
            r.hidden_sum[seq, :, lanes_at(block * width, width)] = jnp.sum(
                value[inner] * valid_of(seq), axis=0, keepdims=True
            )
        acc[span, :] += jnp.dot(
            (value * gain_at(block)).astype(BF16),
            head_w[rows_at(block * width, width), :],
            preferred_element_type=F32,
        )

    mixture = mixture_all.at[dp_me]

    def attend(group):
        whole = span_of(group)
        inv_rms = lax.rsqrt(
            jnp.sum(squares[whole, :], axis=1, keepdims=True) * (1.0 / width_all) + EPSILON
        )
        r.inv_ref[whole, :] = inv_rms
        for seq, inner, span in sequences(group):
            inverse = inv_rms[inner]
            query = jnp.concatenate(
                [
                    rotary(acc[span, g * HEAD : (g + 1) * HEAD] * inverse, table, 1.0)
                    for g in range(groups)
                ],
                axis=0,
            ).astype(BF16)
            key = rotary(acc[span, query_cols : query_cols + kv_cols] * inverse, table, 1.0)
            key = key.astype(BF16)
            value = (acc[span, query_cols + kv_cols :] * inverse).astype(BF16)
            r.query_ref[seq] = query
            r.key_ref[seq] = key
            r.value_ref[seq] = value
            scores = contract_last(query, key) * HEAD ** (-0.5)
            place = lax.broadcasted_iota(jnp.int32, scores.shape, 0) % length
            scores = jnp.where(
                place >= lax.broadcasted_iota(jnp.int32, scores.shape, 1), scores, -1e30
            )
            weights = jnp.exp(scores - jnp.max(scores, axis=1, keepdims=True))
            weights = weights / jnp.sum(weights, axis=1, keepdims=True)
            r.prob_ref[seq] = weights
            mixed = jnp.dot(weights.astype(BF16), value, preferred_element_type=F32).astype(BF16)
            for g in range(groups):
                mixture[span, g * HEAD : (g + 1) * HEAD] = mixed[g * length : (g + 1) * length]
        if group == 0:

            @pl.when(jnp.logical_not(forth.has_source))
            def _():
                pl.semaphore_wait(barrier, expected)

            loads[3].wait()

    def part(group, block):
        return jnp.dot(mixture[span_of(group), :], out_columns(block), preferred_element_type=F32)

    def finish(group, block, total):
        return (hidden[group * blocks + block].astype(F32) + total).astype(BF16)

    ins = [
        StreamIn(
            forth,
            group,
            hidden,
            (r.relay_s, r.relay_r),
            (r.in_far_s, r.in_far_r),
            (r.in_near_s, r.in_near_r),
        )
        for group in range(2)
    ]
    outs = [
        StreamOut(
            forth,
            group,
            part,
            finish,
            hidden,
            (r.near_send, r.near_got, r.far_send, r.far_got, r.relay_send, r.keep),
            (r.relay_s, r.relay_r),
            (r.out_far_s, r.out_far_r),
            (r.out_near_s, r.out_near_r),
        )
        for group in range(2)
    ]
    run_pass(
        FORWARD_ORDER, ins, outs, forth.has_source, forth.has_target, consume, attend, lambda group: None, None
    )

    mixture_sum = jnp.dot(r.pool_ref[...], mixture[...], preferred_element_type=F32)
    coarse = mixture_sum.astype(BF16)
    fine = (mixture_sum - coarse.astype(F32)).astype(BF16)
    both = jnp.concatenate([coarse, fine], axis=0)
    first = (mp_me == 0).astype(F32)
    pooled = r.pooled

    def pool_block(block, carry):
        sums = jnp.dot(both, out_columns(block), preferred_element_type=F32)
        sums = sums[: pool_shape[0]] + sums[pool_shape[0] :]
        lines = [
            (sums[seq : seq + 1] + first * r.hidden_sum[seq, :, lanes_at(block * width, width)])
            / count_of(seq).astype(F32)
            for seq in range(seq_count)
        ]
        pooled[me, :, lanes_at(block * width, width)] = jnp.concatenate(lines, axis=0)
        return carry

    lax.fori_loop(0, blocks, pool_block, 0, unroll=4)

    def pool_copy(shift):
        to_dp, to_mp, _ = peer(shift)
        return pltpu.make_async_remote_copy(
            src_ref=pooled.at[me],
            dst_ref=pooled.at[me],
            send_sem=r.pool_s.at[shift],
            recv_sem=r.pool_r.at[me],
            device_id={"dp": to_dp, "mp": to_mp},
            device_id_type=MESH,
        )

    def pool_arrival(shift):
        from_dp, from_mp, spot = peer(shift)
        return pltpu.make_async_remote_copy(
            src_ref=pooled.at[spot],
            dst_ref=pooled.at[spot],
            send_sem=r.pool_s.at[shift],
            recv_sem=r.pool_r.at[spot],
            device_id={"dp": from_dp, "mp": from_mp},
            device_id_type=MESH,
        )

    for shift in range(1, members):
        pool_copy(shift).start()

    def to_owner(source, target, sems, group, block):
        step = lax.rem(block, share)
        return pltpu.make_async_remote_copy(
            src_ref=source.at[group * blocks + block],
            dst_ref=target.at[dp_me, step, pl.ds(group * rows, rows)],
            send_sem=sems[0].at[group * blocks + block],
            recv_sem=sems[1].at[dp_me, group * share + step],
            device_id={"dp": block // share},
            device_id_type=MESH,
        )

    def from_member(target, sems, member, group, step):
        piece = target.at[member, step, pl.ds(group * rows, rows)]
        return pltpu.make_async_remote_copy(
            src_ref=piece,
            dst_ref=piece,
            send_sem=sems[0].at[0],
            recv_sem=sems[1].at[member, group * share + step],
            device_id={"dp": member},
            device_id_type=MESH,
        )

    def rows_copy(target, sems, shift, group, own):
        other = lax.rem(dp_me + shift, dp_count)
        member = dp_me if own else other
        piece = target.at[member, pl.ds(group * rows, rows)]
        return pltpu.make_async_remote_copy(
            src_ref=piece,
            dst_ref=piece,
            send_sem=sems[0].at[group * dp_count + shift],
            recv_sem=sems[1].at[group * dp_count + member],
            device_id={"dp": other},
            device_id_type=MESH,
        )

    def hand_out(value, spare, target, sems, group, block):
        mine = block // share == dp_me

        @pl.when(mine)
        def _():
            target[dp_me, lax.rem(block, share), span_of(group), :] = value

        @pl.when(jnp.logical_not(mine))
        def _():
            spare[group * blocks + block] = value
            to_owner(spare, target, sems, group, block).start()

    def hand_out_normed():
        for group in range(2):

            def normed_block(block, carry, group=group):
                value = hidden[group * blocks + block].astype(F32) * r.inv_ref[span_of(group), :]
                value = (value * gain_at(block)).astype(BF16)
                hand_out(value, r.normed_out, normed_all, normed_sems, group, block)
                return carry

            lax.fori_loop(0, blocks, normed_block, 0, unroll=2)
            for shift in range(1, dp_count):
                rows_copy(mixture_all, mixture_sems, shift, group, True).start()

    pl.when(back.has_source)(hand_out_normed)
    for shift in range(1, members):
        pool_arrival(shift).wait_recv()
    embedded = []
    for member in range(dp_count):
        total = pooled[member * mp_count]
        for other in range(1, mp_count):
            total = total + pooled[member * mp_count + other]
        embedded.append(total)
    pairs = dp_count * pair_count
    queries = jnp.concatenate(
        [embedded[p // pair_count][2 * (p % pair_count) :][:1] for p in range(pairs)], axis=0
    )
    passages = jnp.concatenate(
        [embedded[p // pair_count][2 * (p % pair_count) + 1 :][:1] for p in range(pairs)], axis=0
    )
    partner = lax.broadcasted_iota(jnp.int32, (pairs, pairs), 1)
    line = lax.broadcasted_iota(jnp.int32, (pairs, pairs), 0)
    target = jnp.zeros((pairs, pairs), F32)
    for p in range(pairs):
        target = jnp.where(jnp.logical_and(line == p, partner == positives[p]), 1.0, target)
    losses, query_slopes, passage_slopes = matryoshka(queries, passages, target)
    lane = lax.broadcasted_iota(jnp.int32, (1, 128), 1)
    packed = jnp.zeros((1, 128), F32)
    for level in range(WIDTHS):
        packed = jnp.where(lane == level, losses[level], packed)
    losses_out[...] = packed[:, :WIDTHS]
    slopes = r.slopes
    for p in range(pairs):
        slopes[2 * p] = query_slopes[p : p + 1]
        slopes[2 * p + 1] = passage_slopes[p : p + 1]

    grad_in, mix_grad = r.grad_in, r.mix_grad

    def upstream(group, block):
        tokens = [
            valid_of(seq)
            / count_of(seq).astype(F32)
            * slopes[dp_me * seq_count + seq, :, lanes_at(block * width, width)]
            for seq, _, _ in sequences(group)
        ]
        tokens = tokens[0] if pair_count == 1 else jnp.concatenate(tokens, axis=0)
        return tokens + grad_in[group * blocks + block].astype(F32)

    def consume_back(group, block):
        outer = upstream(group, block).astype(BF16)
        hand_out(outer, outer_out, outer_all, outer_sems, group, block)
        mix_grad[span_of(group), :] += contract_last(outer, out_columns(block))

    head_grads = heads_all.at[dp_me]
    row_dots = r.row_dots
    diagonal = lax.broadcasted_iota(jnp.int32, (rows, row_pad), 0) == lax.broadcasted_iota(
        jnp.int32, (rows, row_pad), 1
    )

    def dots_copy(shift, group, own):
        other = lax.rem(mp_me + shift, mp_count)
        member = mp_me if own else other
        piece = row_dots.at[group * mp_count + member]
        return pltpu.make_async_remote_copy(
            src_ref=piece,
            dst_ref=piece,
            send_sem=r.dots_s.at[group * mp_count + shift],
            recv_sem=r.dots_r.at[group * mp_count + member],
            device_id={"mp": other},
            device_id_type=MESH,
        )

    def attend_back(group):
        row_dot = []
        for seq, _, span in sequences(group):
            mixed = jnp.concatenate(
                [mix_grad[span, g * HEAD : (g + 1) * HEAD] for g in range(groups)], axis=0
            ).astype(BF16)
            weights = r.prob_ref[seq]
            value_grad = contract_rows(weights.astype(BF16), mixed).astype(BF16)
            pulled = contract_last(mixed, r.value_ref[seq]).astype(BF16).astype(F32)
            score_grad = weights * (pulled - jnp.sum(weights * pulled, axis=1, keepdims=True))
            score_grad = (score_grad * HEAD ** (-0.5)).astype(BF16)
            query_grad = jnp.dot(score_grad, r.key_ref[seq], preferred_element_type=F32)
            query_grad = query_grad.astype(BF16).astype(F32)
            key_grad = contract_rows(score_grad, r.query_ref[seq]).astype(BF16).astype(F32)
            pieces = [
                rotary(query_grad[g * length : (g + 1) * length], table, -1.0).astype(BF16)
                for g in range(groups)
            ]
            pieces = pieces + [rotary(key_grad, table, -1.0).astype(BF16), value_grad]
            joined = jnp.concatenate(pieces, axis=1)
            head_grads[span, :] = joined
            row_dot.append(lane_sum(joined.astype(F32) * acc[span, :]))
        for shift in range(1, dp_count):
            rows_copy(heads_all, heads_sems, shift, group, True).start()
        row_dot = row_dot[0] if pair_count == 1 else jnp.concatenate(row_dot, axis=0)

        @pl.when(back.has_target)
        def _():
            row_dots[group * mp_count + mp_me] = jnp.sum(
                jnp.where(diagonal, row_dot, 0.0), axis=0, keepdims=True
            )
            for shift in range(1, mp_count):
                dots_copy(shift, group, True).start()

    def part_back(group, block):
        span = span_of(group)
        value = contract_last(head_grads[span, :], head_w[rows_at(block * width, width), :])
        scaled = value * (hidden[group * blocks + block].astype(F32) * r.inv_ref[span, :])
        r.gain_part[:, lanes_at(block * width, width)] += jnp.sum(scaled, axis=0, keepdims=True)
        return value

    def prepare(group):
        for shift in range(1, mp_count):
            dots_copy(shift, group, False).wait_recv()
        total = row_dots[group * mp_count]
        for member in range(1, mp_count):
            total = total + row_dots[group * mp_count + member]
        inverse = r.inv_ref[span_of(group), :]
        r.pull_ref[span_of(group), :] = (
            lane_sum(jnp.where(diagonal, total, 0.0))
            * inverse
            * inverse
            * inverse
            * (1.0 / width_all)
        )

    def finish_back(group, block, total):
        span = span_of(group)
        value = upstream(group, block) + total * gain_at(block) * r.inv_ref[span, :]
        pulled = hidden[group * blocks + block].astype(F32) * r.pull_ref[span, :]
        return (value - pulled).astype(BF16)

    def gain_only(group):
        def body(block, carry):
            part_back(group, block)
            return carry

        lax.fori_loop(0, blocks, body, 0, unroll=2)

    ins_back = [
        StreamIn(
            back,
            group,
            grad_in,
            (r.relay_sb, r.relay_rb),
            (r.in_far_sb, r.in_far_rb),
            (r.in_near_sb, r.in_near_rb),
        )
        for group in range(2)
    ]
    outs_back = [
        StreamOut(
            back,
            group,
            part_back,
            finish_back,
            grad_in,
            (r.near_send_b, r.near_got_b, r.far_send_b, r.far_got_b, r.relay_send_b, r.keep_b),
            (r.relay_sb, r.relay_rb),
            (r.out_far_sb, r.out_far_rb),
            (r.out_near_sb, r.out_near_rb),
        )
        for group in range(2)
    ]
    run_pass(
        BACKWARD_ORDER,
        ins_back,
        outs_back,
        back.has_source,
        back.has_target,
        consume_back,
        attend_back,
        prepare,
        gain_only,
    )

    pl.when(jnp.logical_not(back.has_source))(hand_out_normed)

    gain_got = r.gain_got
    gain_cols = gain_got.shape[2]

    def gain_copy(shift):
        to_dp, to_mp, spot = peer(shift)
        return pltpu.make_async_remote_copy(
            src_ref=r.gain_part.at[:, lanes_at(spot * gain_cols, gain_cols)],
            dst_ref=gain_got.at[me],
            send_sem=r.gain_s.at[shift],
            recv_sem=r.gain_r.at[me],
            device_id={"dp": to_dp, "mp": to_mp},
            device_id_type=MESH,
        )

    def gain_arrival(shift):
        from_dp, from_mp, spot = peer(shift)
        return pltpu.make_async_remote_copy(
            src_ref=gain_got.at[spot],
            dst_ref=gain_got.at[spot],
            send_sem=r.gain_s.at[shift],
            recv_sem=r.gain_r.at[spot],
            device_id={"dp": from_dp, "mp": from_mp},
            device_id_type=MESH,
        )

    for shift in range(1, members):
        gain_copy(shift).start()
    drain_pass(ins, outs, forth.has_source, forth.has_target)
    drain_pass(ins_back, outs_back, back.has_source, back.has_target)

    @pl.when(back.has_target)
    def _():
        for group in range(2):
            for shift in range(1, mp_count):
                dots_copy(shift, group, True).wait_send()

    total = r.gain_part[:, lanes_at(me * gain_cols, gain_cols)]
    for shift in range(1, members):
        gain_arrival(shift).wait_recv()
        total = total + gain_got[lax.rem(me + shift, members)]
    gain_out[...] = total

    for shift in range(1, members):
        pool_copy(shift).wait_send()
        gain_copy(shift).wait_send()
    for group in range(2):
        for shift in range(1, dp_count):
            rows_copy(mixture_all, mixture_sems, shift, group, True).wait_send()
            rows_copy(heads_all, heads_sems, shift, group, True).wait_send()
            rows_copy(mixture_all, mixture_sems, shift, group, False).wait_recv()
            rows_copy(heads_all, heads_sems, shift, group, False).wait_recv()

        def drain(block, carry, group=group):
            @pl.when(block // share != dp_me)
            def _():
                to_owner(r.normed_out, normed_all, normed_sems, group, block).wait_send()
                to_owner(outer_out, outer_all, outer_sems, group, block).wait_send()

            return carry

        lax.fori_loop(0, blocks, drain, 0)
        for shift in range(1, dp_count):
            member = lax.rem(dp_me + shift, dp_count)
            for step in range(share):
                from_member(normed_all, normed_sems, member, group, step).wait_recv()
                from_member(outer_all, outer_sems, member, group, step).wait_recv()


def step_pass(lengths, positives, entrance, gain, table, wq, wk, wv, wo):
    rows, width_all = entrance.shape
    dp_count, mp_count = lax.axis_size("dp"), lax.axis_size("mp")
    members = dp_count * mp_count
    blocks = mp_count * SUB
    width = width_all // blocks
    share = blocks // dp_count
    seq_count = 2 * lengths.shape[0]
    length = rows // seq_count
    query_cols = wq.shape[1]
    head_cols = query_cols + wk.shape[1] + wv.shape[1]
    stacked = query_cols // HEAD * length
    row_pad = -(-(rows // 2) // 128) * 128
    pool_rows = -(-seq_count // 16) * 16
    dma = pltpu.SemaphoreType.DMA
    block = (rows // 2, width)
    shapes = dict(
        head_w=((width_all, head_cols), BF16),
        out_w=(wo.shape, BF16),
        acc=((rows, head_cols), F32),
        squares=((rows, 128), F32),
        inv_ref=((rows, 1), F32),
        pull_ref=((rows, 1), F32),
        query_ref=((seq_count, stacked, HEAD), BF16),
        key_ref=((seq_count, length, HEAD), BF16),
        value_ref=((seq_count, length, HEAD), BF16),
        prob_ref=((seq_count, stacked, length), F32),
        pooled=((members, seq_count, width_all), F32),
        hidden_sum=((seq_count, 1, width_all), F32),
        slopes=((dp_count * seq_count, 1, width_all), F32),
        normed_out=((2 * blocks, *block), BF16),
        outer_out=((2 * blocks, *block), BF16),
        grad_in=((2 * blocks, *block), BF16),
        mix_grad=((rows, query_cols), F32),
        row_dots=((2 * mp_count, 1, row_pad), F32),
        gain_part=((1, width_all), F32),
        gain_got=((members, 1, width_all // members), F32),
        pool_ref=((pool_rows, rows), BF16),
        near_send=((4 * SUB, *block), BF16),
        near_got=((4 * SUB, *block), BF16),
        far_send=((2 * SUB, *block), BF16),
        far_got=((2 * SUB, *block), BF16),
        relay_send=((2 * SUB, *block), BF16),
        keep=((2 * SUB, *block), F32),
        near_send_b=((4 * SUB, *block), BF16),
        near_got_b=((4 * SUB, *block), BF16),
        far_send_b=((2 * SUB, *block), BF16),
        far_got_b=((2 * SUB, *block), BF16),
        relay_send_b=((2 * SUB, *block), BF16),
        keep_b=((2 * SUB, *block), F32),
    )
    counts = dict(
        load_sem=(4,),
        enter_sem=(2 * blocks,),
        pool_s=(members,),
        pool_r=(members,),
        normed_s=(2 * blocks,),
        normed_r=(dp_count, 2 * share),
        outer_s=(2 * blocks,),
        outer_r=(dp_count, 2 * share),
        mixture_s=(2 * dp_count,),
        mixture_r=(2 * dp_count,),
        heads_s=(2 * dp_count,),
        heads_r=(2 * dp_count,),
        dots_s=(2 * mp_count,),
        dots_r=(2 * mp_count,),
        gain_s=(members,),
        gain_r=(members,),
        relay_s=(2 * SUB,),
        in_far_s=(2 * SUB,),
        out_far_s=(2 * SUB,),
        in_near_s=(4 * SUB,),
        out_near_s=(4 * SUB,),
        relay_r=(2 * SUB,),
        in_far_r=(2 * SUB,),
        out_far_r=(2 * SUB,),
        in_near_r=(4 * SUB,),
        out_near_r=(4 * SUB,),
        relay_sb=(2 * SUB,),
        in_far_sb=(2 * SUB,),
        out_far_sb=(2 * SUB,),
        in_near_sb=(4 * SUB,),
        out_near_sb=(4 * SUB,),
        relay_rb=(2 * SUB,),
        in_far_rb=(2 * SUB,),
        out_far_rb=(2 * SUB,),
        in_near_rb=(4 * SUB,),
        out_near_rb=(4 * SUB,),
    )
    scratch = Scratch(
        **{name: pltpu.VMEM(*shape) for name, shape in shapes.items()},
        **{name: dma(count) for name, count in counts.items()},
    )
    vmem = pl.BlockSpec(memory_space=pltpu.VMEM)
    smem = pl.BlockSpec(memory_space=pltpu.SMEM)
    hbm = pl.BlockSpec(memory_space=pltpu.HBM)
    return pl.pallas_call(
        step_kernel,
        out_shape=(
            jax.ShapeDtypeStruct((1, WIDTHS), F32),
            jax.ShapeDtypeStruct((1, width_all // members), F32),
            jax.ShapeDtypeStruct((dp_count, share, rows, width), BF16),
            jax.ShapeDtypeStruct((dp_count, rows, query_cols), BF16),
            jax.ShapeDtypeStruct((dp_count, share, rows, width), BF16),
            jax.ShapeDtypeStruct((dp_count, rows, head_cols), BF16),
        ),
        in_specs=[smem, smem, hbm, vmem, vmem, hbm, hbm, hbm, hbm],
        out_specs=(vmem,) * 6,
        scratch_shapes=[pltpu.VMEM((2 * blocks, *block), BF16)] + list(scratch),
        compiler_params=pltpu.CompilerParams(
            collective_id=0, has_side_effects=True, vmem_limit_bytes=56 * 1024 * 1024
        ),
        name="step_pass",
    )(lengths, positives, entrance, gain, table, wq, wk, wv, wo)


def weight_kernel(
    normed, mixture, outer, heads, query_grad, key_grad, value_grad, out_grad, turned
):
    members, rows = heads.shape[:2]
    query_cols, kv_cols = query_grad.shape[1], key_grad.shape[1]

    @pl.when(pl.program_id(0) == 0)
    def _():
        for member in range(members):
            turned[:, member * rows : (member + 1) * rows] = mixture[member].T

    inputs = jnp.concatenate([normed[member, 0] for member in range(members)], axis=0)
    grads = jnp.concatenate([heads[member] for member in range(members)], axis=0)
    product = contract_rows(inputs, grads)
    query_grad[...] = product[:, :query_cols]
    key_grad[...] = product[:, query_cols : query_cols + kv_cols]
    value_grad[...] = product[:, query_cols + kv_cols :]
    grads = jnp.concatenate([outer[member, 0] for member in range(members)], axis=0)
    out_grad[...] = jnp.dot(turned[...], grads, preferred_element_type=F32)


def weight_grads(normed, mixture, outer, heads, query_cols, kv_cols):
    members, share, rows, width = normed.shape
    columns = share * width
    streamed = pl.BlockSpec((members, 1, rows, width), lambda step: (0, step, 0, 0))
    vmem = pl.BlockSpec(memory_space=pltpu.VMEM)

    def tall(cols):
        return pl.BlockSpec((width, cols), lambda step: (step, 0))

    return pl.pallas_call(
        weight_kernel,
        grid=(share,),
        in_specs=[streamed, vmem, streamed, vmem],
        out_specs=(
            tall(query_cols),
            tall(kv_cols),
            tall(kv_cols),
            pl.BlockSpec((query_cols, width), lambda step: (0, step)),
        ),
        out_shape=(
            pltpu.HBM((columns, query_cols), F32),
            pltpu.HBM((columns, kv_cols), F32),
            pltpu.HBM((columns, kv_cols), F32),
            pltpu.HBM((query_cols, columns), F32),
        ),
        scratch_shapes=[pltpu.VMEM((query_cols, members * rows), BF16)],
        compiler_params=pltpu.CompilerParams(dimension_semantics=("arbitrary",)),
        name="weight_grads",
    )(normed, mixture, outer, heads)


def local(entrance, lengths, positives, norm_gains, query_proj, key_proj, value_proj, out_proj):
    length = entrance.shape[2]
    width_all = entrance.shape[3]
    query_cols = query_proj.shape[2]
    kv_cols = key_proj.shape[2]
    losses, gain_share, normed, mixture, outer, heads = step_pass(
        lengths,
        positives,
        entrance.reshape(-1, width_all),
        norm_gains,
        jnp.asarray(rotary_constants(length)),
        query_proj[0],
        key_proj[0],
        value_proj[0],
        out_proj[0],
    )
    query_grad, key_grad, value_grad, out_grad = weight_grads(
        normed, mixture, outer, heads, query_cols, kv_cols
    )
    return (
        losses,
        gain_share,
        query_grad[None],
        key_grad[None],
        value_grad[None],
        out_grad[None],
    )


def solution(mesh):
    in_specs = (
        P("dp", None, None, None),
        P("dp", None),
        P(),
        P("section", None),
        P("section", None, "mp"),
        P("section", None, "mp"),
        P("section", None, "mp"),
        P("section", "mp", None),
    )
    out_specs = (
        P("section", None),
        P("section", ("dp", "mp")),
        P("section", "dp", "mp"),
        P("section", "dp", "mp"),
        P("section", "dp", "mp"),
        P("section", "mp", "dp"),
    )
    return jax.shard_map(local, mesh=mesh, in_specs=in_specs, out_specs=out_specs, check_vma=False)
```

time: 216 us -> 170 us (0.79)
  Pallas kernels: 212 us -> 167 us
    pallas_call x1, Pallas kernels: 203 us -> 157 us  [step_pass(): pl.pallas_call(step_kernel, out_shape=(jax.ShapeDtypeStruct((1, WIDTHS),...]
where the time goes in v3:
time: 170 us
  Pallas kernels  167 us (98%)
  local copies, waits for them, and re-layouts  2.35 us (1%)
    pallas_call x1, Pallas kernels, step_pass(): pl.pallas_call(step_kernel, out_shape=(jax.ShapeDtypeStruct((1, WIDTHS),...  157 us
    pallas_call x1, Pallas kernels, weight_grads(): pl.pallas_call(weight_kernel, grid=(share,), in_specs=[streamed, vmem, st...  9.9 us

profile of v3, /device:TPU:0, one launch (start us, length us, event | category | flops | bytes accessed | tf_op | source)
XLA Modules:
  0.0 170.1 jit_solution(12734201041241746550)
XLA Ops:
  0.6 157.2 %step_pass.1 = (f32[1,7]{1,0:T(1,128)}, f32[1,512]{1,0:T(1,128)}, bf16[2,8,192,256]{3,2,1,0:T(8,128)(2,1)}, bf16[2,192,512]{2,1,0:T(8,128)(2,1)}, bf16[2,8,192,2...) custom-call(s32[1,2]{1,0:T(1,128)} %lengths.1, s32[2]{0:T(128)} %positives.1, bf16[192,4096]{1,0:T(8,128)(2,1)} %bitcast.11, ...), custom_call_target="tpu_custom_call" | custom-call | tf_op jit(solution)/shard_map/step_pass/pallas_call | solution.py:1151
  157.9 9.9 %weight_grads.1 = (f32[2048,512]{1,0:T(8,128)}, f32[2048,128]{1,0:T(8,128)}, f32[2048,128]{1,0:T(8,128)}, f32[512,2048]{1,0:T(8,128)}) custom-call(bf16[2,8,192,256]{3,2,1,0:T(8,128)(2,1)} %get-tuple-element.18.normed, bf16[2,192,512]{2,1,0:T(8,128)(2,1)} %get-tuple-element.19.mixture, bf16[2,8,192,256]{3,2,1,0:T(8,128)(2,1)} %get-tuple-element.20.outer, ...), custom_call_target="tpu_custom_call" | custom-call | tf_op jit(solution)/shard_map/weight_grads/pallas_call | solution.py:1201
  167.8 1.1 copy.17
  168.9 1.2 copy.18

commit v4 on v3

--- a/solution.py
+++ b/solution.py
@@ -462,6 +462,8 @@
     heads_r: object
     dots_s: object
     dots_r: object
+    pass_s: object
+    pass_r: object
     gain_s: object
     gain_r: object
 
@@ -513,6 +515,9 @@
     def span_of(group):
         return slice(group * rows, (group + 1) * rows)
 
+    def member_rows(member, group):
+        return rows_at((member * 2 + group) * rows, rows)
+
     def sequences(group):
         for local_seq in range(pair_count):
             inner = slice(local_seq * length, (local_seq + 1) * length)
@@ -588,7 +593,7 @@
     picks = jnp.zeros(pool_shape, F32)
     for seq in range(seq_count):
         inside = jnp.logical_and(column >= seq * length, column < seq * length + count_of(seq))
-        picks = jnp.where(jnp.logical_and(line == seq, inside), 1.0, picks)
+        picks = jnp.where(jnp.logical_and(line == seq % pair_count, inside), 1.0, picks)
     r.pool_ref[...] = picks.astype(BF16)
     for load in loads[:3]:
         load.wait()
@@ -626,7 +631,7 @@
             preferred_element_type=F32,
         )
 
-    mixture = mixture_all.at[dp_me]
+    mixture = mixture_all.at[pl.ds(pl.multiple_of(dp_me * 2 * rows, ROW_TILE), 2 * rows)]
 
     def attend(group):
         whole = span_of(group)
@@ -668,6 +673,44 @@
 
             loads[3].wait()
 
+    first = (mp_me == 0).astype(F32)
+    pooled = r.pooled
+
+    def pool_copy(group, shift, own):
+        other_dp, other_mp, spot = peer(shift)
+        member = group * members + (me if own else spot)
+        return pltpu.make_async_remote_copy(
+            src_ref=pooled.at[member],
+            dst_ref=pooled.at[member],
+            send_sem=r.pool_s.at[group * members + shift],
+            recv_sem=r.pool_r.at[member],
+            device_id={"dp": other_dp, "mp": other_mp},
+            device_id_type=MESH,
+        )
+
+    def send_pooled(group):
+        span = span_of(group)
+        mixture_sum = jnp.dot(r.pool_ref[:, span], mixture[span, :], preferred_element_type=F32)
+        coarse = mixture_sum.astype(BF16)
+        fine = (mixture_sum - coarse.astype(F32)).astype(BF16)
+        both = jnp.concatenate([coarse, fine], axis=0)
+
+        def pool_block(block, carry):
+            sums = jnp.dot(both, out_columns(block), preferred_element_type=F32)
+            sums = sums[: pool_shape[0]] + sums[pool_shape[0] :]
+            lines = [
+                (sums[line : line + 1] + first * r.hidden_sum[seq, :, lanes_at(block * width, width)])
+                / count_of(seq).astype(F32)
+                for line, (seq, _, _) in enumerate(sequences(group))
+            ]
+            lines = lines[0] if pair_count == 1 else jnp.concatenate(lines, axis=0)
+            pooled[group * members + me, :, lanes_at(block * width, width)] = lines
+            return carry
+
+        lax.fori_loop(0, blocks, pool_block, 0, unroll=4)
+        for shift in range(1, members):
+            pool_copy(group, shift, True).start()
+
     def part(group, block):
         return jnp.dot(mixture[span_of(group), :], out_columns(block), preferred_element_type=F32)
 
@@ -700,59 +743,19 @@
         for group in range(2)
     ]
     run_pass(
-        FORWARD_ORDER, ins, outs, forth.has_source, forth.has_target, consume, attend, lambda group: None, None
-    )
-
-    mixture_sum = jnp.dot(r.pool_ref[...], mixture[...], preferred_element_type=F32)
-    coarse = mixture_sum.astype(BF16)
-    fine = (mixture_sum - coarse.astype(F32)).astype(BF16)
-    both = jnp.concatenate([coarse, fine], axis=0)
-    first = (mp_me == 0).astype(F32)
-    pooled = r.pooled
-
-    def pool_block(block, carry):
-        sums = jnp.dot(both, out_columns(block), preferred_element_type=F32)
-        sums = sums[: pool_shape[0]] + sums[pool_shape[0] :]
-        lines = [
-            (sums[seq : seq + 1] + first * r.hidden_sum[seq, :, lanes_at(block * width, width)])
-            / count_of(seq).astype(F32)
-            for seq in range(seq_count)
-        ]
-        pooled[me, :, lanes_at(block * width, width)] = jnp.concatenate(lines, axis=0)
-        return carry
-
-    lax.fori_loop(0, blocks, pool_block, 0, unroll=4)
-
-    def pool_copy(shift):
-        to_dp, to_mp, _ = peer(shift)
-        return pltpu.make_async_remote_copy(
-            src_ref=pooled.at[me],
-            dst_ref=pooled.at[me],
-            send_sem=r.pool_s.at[shift],
-            recv_sem=r.pool_r.at[me],
-            device_id={"dp": to_dp, "mp": to_mp},
-            device_id_type=MESH,
-        )
-
-    def pool_arrival(shift):
-        from_dp, from_mp, spot = peer(shift)
-        return pltpu.make_async_remote_copy(
-            src_ref=pooled.at[spot],
-            dst_ref=pooled.at[spot],
-            send_sem=r.pool_s.at[shift],
-            recv_sem=r.pool_r.at[spot],
-            device_id={"dp": from_dp, "mp": from_mp},
-            device_id_type=MESH,
-        )
-
-    for shift in range(1, members):
-        pool_copy(shift).start()
+        FORWARD_ORDER, ins, outs, forth.has_source, forth.has_target, consume, attend, lambda group: None, send_pooled
+    )
+
+    @pl.when(forth.has_target)
+    def _():
+        for group in range(2):
+            send_pooled(group)
 
     def to_owner(source, target, sems, group, block):
         step = lax.rem(block, share)
         return pltpu.make_async_remote_copy(
             src_ref=source.at[group * blocks + block],
-            dst_ref=target.at[dp_me, step, pl.ds(group * rows, rows)],
+            dst_ref=target.at[step, member_rows(dp_me, group)],
             send_sem=sems[0].at[group * blocks + block],
             recv_sem=sems[1].at[dp_me, group * share + step],
             device_id={"dp": block // share},
@@ -760,7 +763,7 @@
         )
 
     def from_member(target, sems, member, group, step):
-        piece = target.at[member, step, pl.ds(group * rows, rows)]
+        piece = target.at[step, member_rows(member, group)]
         return pltpu.make_async_remote_copy(
             src_ref=piece,
             dst_ref=piece,
@@ -773,7 +776,7 @@
     def rows_copy(target, sems, shift, group, own):
         other = lax.rem(dp_me + shift, dp_count)
         member = dp_me if own else other
-        piece = target.at[member, pl.ds(group * rows, rows)]
+        piece = target.at[member_rows(member, group)]
         return pltpu.make_async_remote_copy(
             src_ref=piece,
             dst_ref=piece,
@@ -783,14 +786,18 @@
             device_id_type=MESH,
         )
 
-    def hand_out(value, spare, target, sems, group, block):
+    def hand_out(value, spare, target, sems, group, block, passes=None):
         mine = block // share == dp_me
 
         @pl.when(mine)
         def _():
-            target[dp_me, lax.rem(block, share), span_of(group), :] = value
-
-        @pl.when(jnp.logical_not(mine))
+            target[lax.rem(block, share), member_rows(dp_me, group), :] = value
+
+        sends = jnp.logical_not(mine)
+        if passes is not None:
+            sends = jnp.logical_and(sends, passes)
+
+        @pl.when(sends)
         def _():
             spare[group * blocks + block] = value
             to_owner(spare, target, sems, group, block).start()
@@ -809,21 +816,26 @@
                 rows_copy(mixture_all, mixture_sems, shift, group, True).start()
 
     pl.when(back.has_source)(hand_out_normed)
-    for shift in range(1, members):
-        pool_arrival(shift).wait_recv()
+    for group in range(2):
+        for shift in range(1, members):
+            pool_copy(group, shift, False).wait_recv()
     embedded = []
-    for member in range(dp_count):
-        total = pooled[member * mp_count]
-        for other in range(1, mp_count):
-            total = total + pooled[member * mp_count + other]
-        embedded.append(total)
+    for group in range(2):
+        for member in range(dp_count):
+            start = group * members + member * mp_count
+            total = pooled[start]
+            for other in range(1, mp_count):
+                total = total + pooled[start + other]
+            embedded.append(total)
     pairs = dp_count * pair_count
-    queries = jnp.concatenate(
-        [embedded[p // pair_count][2 * (p % pair_count) :][:1] for p in range(pairs)], axis=0
-    )
-    passages = jnp.concatenate(
-        [embedded[p // pair_count][2 * (p % pair_count) + 1 :][:1] for p in range(pairs)], axis=0
-    )
+
+    def embedding(seq):
+        member, inner = seq // seq_count, seq % seq_count
+        block = embedded[inner // pair_count * dp_count + member]
+        return block[inner % pair_count :][:1]
+
+    queries = jnp.concatenate([embedding(2 * p) for p in range(pairs)], axis=0)
+    passages = jnp.concatenate([embedding(2 * p + 1) for p in range(pairs)], axis=0)
     partner = lax.broadcasted_iota(jnp.int32, (pairs, pairs), 1)
     line = lax.broadcasted_iota(jnp.int32, (pairs, pairs), 0)
     target = jnp.zeros((pairs, pairs), F32)
@@ -854,10 +866,11 @@
 
     def consume_back(group, block):
         outer = upstream(group, block).astype(BF16)
-        hand_out(outer, outer_out, outer_all, outer_sems, group, block)
+        passes = lax.rem(block, 2) == forth.low
+        hand_out(outer, outer_out, outer_all, outer_sems, group, block, passes)
         mix_grad[span_of(group), :] += contract_last(outer, out_columns(block))
 
-    head_grads = heads_all.at[dp_me]
+    head_grads = heads_all.at[pl.ds(pl.multiple_of(dp_me * 2 * rows, ROW_TILE), 2 * rows)]
     row_dots = r.row_dots
     diagonal = lax.broadcasted_iota(jnp.int32, (rows, row_pad), 0) == lax.broadcasted_iota(
         jnp.int32, (rows, row_pad), 1
@@ -984,6 +997,17 @@
 
     pl.when(jnp.logical_not(back.has_source))(hand_out_normed)
 
+    def pass_on(member, group, step):
+        piece = outer_all.at[step, member_rows(member, group)]
+        return pltpu.make_async_remote_copy(
+            src_ref=piece,
+            dst_ref=piece,
+            send_sem=r.pass_s.at[member, group * share + step],
+            recv_sem=r.pass_r.at[member, group * share + step],
+            device_id={"mp": forth.near},
+            device_id_type=MESH,
+        )
+
     gain_got = r.gain_got
     gain_cols = gain_got.shape[2]
 
@@ -1011,7 +1035,19 @@
 
     for shift in range(1, members):
         gain_copy(shift).start()
+    for group in range(2):
+        for shift in range(1, dp_count):
+            member = lax.rem(dp_me + shift, dp_count)
+            for pair in range(share // 2):
+                step = 2 * pair + forth.low
+                from_member(outer_all, outer_sems, member, group, step).wait_recv()
+                pass_on(member, group, step).start()
     drain_pass(ins, outs, forth.has_source, forth.has_target)
+    for group in range(2):
+        for shift in range(1, dp_count):
+            member = lax.rem(dp_me + shift, dp_count)
+            for pair in range(share // 2):
+                pass_on(member, group, 2 * pair + 1 - forth.low).wait_recv()
     drain_pass(ins_back, outs_back, back.has_source, back.has_target)
 
     @pl.when(back.has_target)
@@ -1027,7 +1063,8 @@
     gain_out[...] = total
 
     for shift in range(1, members):
-        pool_copy(shift).wait_send()
+        for group in range(2):
+            pool_copy(group, shift, True).wait_send()
         gain_copy(shift).wait_send()
     for group in range(2):
         for shift in range(1, dp_count):
@@ -1037,9 +1074,14 @@
             rows_copy(heads_all, heads_sems, shift, group, False).wait_recv()
 
         def drain(block, carry, group=group):
-            @pl.when(block // share != dp_me)
+            away = block // share != dp_me
+
+            @pl.when(away)
             def _():
                 to_owner(r.normed_out, normed_all, normed_sems, group, block).wait_send()
+
+            @pl.when(jnp.logical_and(away, lax.rem(block, 2) == forth.low))
+            def _():
                 to_owner(outer_out, outer_all, outer_sems, group, block).wait_send()
 
             return carry
@@ -1049,7 +1091,8 @@
             member = lax.rem(dp_me + shift, dp_count)
             for step in range(share):
                 from_member(normed_all, normed_sems, member, group, step).wait_recv()
-                from_member(outer_all, outer_sems, member, group, step).wait_recv()
+            for pair in range(share // 2):
+                pass_on(member, group, 2 * pair + forth.low).wait_send()
 
 
 def step_pass(lengths, positives, entrance, gain, table, wq, wk, wv, wo):
@@ -1079,7 +1122,7 @@
         key_ref=((seq_count, length, HEAD), BF16),
         value_ref=((seq_count, length, HEAD), BF16),
         prob_ref=((seq_count, stacked, length), F32),
-        pooled=((members, seq_count, width_all), F32),
+        pooled=((2 * members, seq_count // 2, width_all), F32),
         hidden_sum=((seq_count, 1, width_all), F32),
         slopes=((dp_count * seq_count, 1, width_all), F32),
         normed_out=((2 * blocks, *block), BF16),
@@ -1106,14 +1149,16 @@
     counts = dict(
         load_sem=(4,),
         enter_sem=(2 * blocks,),
-        pool_s=(members,),
-        pool_r=(members,),
+        pool_s=(2 * members,),
+        pool_r=(2 * members,),
         normed_s=(2 * blocks,),
         normed_r=(dp_count, 2 * share),
         outer_s=(2 * blocks,),
         outer_r=(dp_count, 2 * share),
         mixture_s=(2 * dp_count,),
         mixture_r=(2 * dp_count,),
+        pass_s=(dp_count, 2 * share),
+        pass_r=(dp_count, 2 * share),
         heads_s=(2 * dp_count,),
         heads_r=(2 * dp_count,),
         dots_s=(2 * mp_count,),
@@ -1153,46 +1198,55 @@
         out_shape=(
             jax.ShapeDtypeStruct((1, WIDTHS), F32),
             jax.ShapeDtypeStruct((1, width_all // members), F32),
-            jax.ShapeDtypeStruct((dp_count, share, rows, width), BF16),
-            jax.ShapeDtypeStruct((dp_count, rows, query_cols), BF16),
-            jax.ShapeDtypeStruct((dp_count, share, rows, width), BF16),
-            jax.ShapeDtypeStruct((dp_count, rows, head_cols), BF16),
+            jax.ShapeDtypeStruct((share, dp_count * rows, width), BF16),
+            jax.ShapeDtypeStruct((dp_count * rows, query_cols), BF16),
+            jax.ShapeDtypeStruct((share, dp_count * rows, width), BF16),
+            jax.ShapeDtypeStruct((dp_count * rows, head_cols), BF16),
         ),
         in_specs=[smem, smem, hbm, vmem, vmem, hbm, hbm, hbm, hbm],
         out_specs=(vmem,) * 6,
         scratch_shapes=[pltpu.VMEM((2 * blocks, *block), BF16)] + list(scratch),
         compiler_params=pltpu.CompilerParams(
-            collective_id=0, has_side_effects=True, vmem_limit_bytes=56 * 1024 * 1024
+            collective_id=0, has_side_effects=True, vmem_limit_bytes=36 * 1024 * 1024
         ),
         name="step_pass",
     )(lengths, positives, entrance, gain, table, wq, wk, wv, wo)
 
 
 def weight_kernel(
-    normed, mixture, outer, heads, query_grad, key_grad, value_grad, out_grad, turned
+    normed,
+    mixture,
+    outer,
+    heads,
+    losses,
+    gain_share,
+    query_grad,
+    key_grad,
+    value_grad,
+    out_grad,
+    losses_out,
+    gain_out,
+    turned,
 ):
-    members, rows = heads.shape[:2]
     query_cols, kv_cols = query_grad.shape[1], key_grad.shape[1]
 
     @pl.when(pl.program_id(0) == 0)
     def _():
-        for member in range(members):
-            turned[:, member * rows : (member + 1) * rows] = mixture[member].T
-
-    inputs = jnp.concatenate([normed[member, 0] for member in range(members)], axis=0)
-    grads = jnp.concatenate([heads[member] for member in range(members)], axis=0)
-    product = contract_rows(inputs, grads)
+        turned[...] = mixture[...].T
+        losses_out[...] = losses[...]
+        gain_out[...] = gain_share[...]
+
+    step = pl.program_id(0)
+    product = contract_rows(normed[step], heads[...])
     query_grad[...] = product[:, :query_cols]
     key_grad[...] = product[:, query_cols : query_cols + kv_cols]
     value_grad[...] = product[:, query_cols + kv_cols :]
-    grads = jnp.concatenate([outer[member, 0] for member in range(members)], axis=0)
-    out_grad[...] = jnp.dot(turned[...], grads, preferred_element_type=F32)
-
-
-def weight_grads(normed, mixture, outer, heads, query_cols, kv_cols):
-    members, share, rows, width = normed.shape
+    out_grad[...] = jnp.dot(turned[...], outer[step], preferred_element_type=F32)
+
+
+def weight_grads(normed, mixture, outer, heads, losses, gain_share, query_cols, kv_cols):
+    share, rows, width = normed.shape
     columns = share * width
-    streamed = pl.BlockSpec((members, 1, rows, width), lambda step: (0, step, 0, 0))
     vmem = pl.BlockSpec(memory_space=pltpu.VMEM)
 
     def tall(cols):
@@ -1201,23 +1255,29 @@
     return pl.pallas_call(
         weight_kernel,
         grid=(share,),
-        in_specs=[streamed, vmem, streamed, vmem],
+        in_specs=[vmem] * 6,
         out_specs=(
             tall(query_cols),
             tall(kv_cols),
             tall(kv_cols),
             pl.BlockSpec((query_cols, width), lambda step: (0, step)),
+            vmem,
+            vmem,
         ),
         out_shape=(
             pltpu.HBM((columns, query_cols), F32),
             pltpu.HBM((columns, kv_cols), F32),
             pltpu.HBM((columns, kv_cols), F32),
             pltpu.HBM((query_cols, columns), F32),
+            jax.ShapeDtypeStruct(losses.shape, F32),
+            jax.ShapeDtypeStruct(gain_share.shape, F32),
         ),
-        scratch_shapes=[pltpu.VMEM((query_cols, members * rows), BF16)],
-        compiler_params=pltpu.CompilerParams(dimension_semantics=("arbitrary",)),
+        scratch_shapes=[pltpu.VMEM((query_cols, rows), BF16)],
+        compiler_params=pltpu.CompilerParams(
+            dimension_semantics=("arbitrary",), vmem_limit_bytes=16 * 1024 * 1024
+        ),
         name="weight_grads",
-    )(normed, mixture, outer, heads)
+    )(normed, mixture, outer, heads, losses, gain_share)
 
 
 def local(entrance, lengths, positives, norm_gains, query_proj, key_proj, value_proj, out_proj):
@@ -1236,8 +1296,8 @@
         value_proj[0],
         out_proj[0],
     )
-    query_grad, key_grad, value_grad, out_grad = weight_grads(
-        normed, mixture, outer, heads, query_cols, kv_cols
+    query_grad, key_grad, value_grad, out_grad, losses, gain_share = weight_grads(
+        normed, mixture, outer, heads, losses, gain_share, query_cols, kv_cols
     )
     return (
         losses,

time: 170 us -> 170 us (level)
  Pallas kernels: 167 us -> 158 us
  local copies, waits for them, and re-layouts: 2.35 us -> 11.1 us
    unnamed x2 -> x18, local copies, waits for them, and re-layouts: 2.35 us -> 11.1 us
    pallas_call x1, Pallas kernels: 157 us -> 151 us  [step_pass(): pl.pallas_call(step_kernel, out_shape=(jax.ShapeDtypeStruct((1, WIDTHS),...]
    pallas_call x1, Pallas kernels: 9.9 us -> 6.49 us  [weight_grads(): pl.pallas_call(weight_kernel, grid=(share,), in_specs=[vmem] * 6, out_spe...]
where the time goes in v4:
time: 170 us
  Pallas kernels  158 us (93%)
  local copies, waits for them, and re-layouts  11.1 us (7%)
    pallas_call x1, Pallas kernels, step_pass(): pl.pallas_call(step_kernel, out_shape=(jax.ShapeDtypeStruct((1, WIDTHS),...  151 us
    unnamed x18, local copies, waits for them, and re-layouts  11.1 us
    pallas_call x1, Pallas kernels, weight_grads(): pl.pallas_call(weight_kernel, grid=(share,), in_specs=[vmem] * 6, out_spe...  6.49 us

profile of v4, /device:TPU:0, one launch (start us, length us, event | category | flops | bytes accessed | tf_op | source)
XLA Modules:
  0.0 169.6 jit_solution(4939390625688467895)
XLA Ops:
  0.6 0.0 copy-start
  0.6 2.2 %copy-done = bf16[1,4096,512]{2,1,0:T(8,128)(2,1)S(1)} copy-done((bf16[1,4096,512]{2,1,0:T(8,128)(2,1)S(1)}, bf16[1,4096,512]{2,1,0:T(8,128)(2,1)}, u32[]{:S(2)}) %copy-start) | copy-done | bytes 4194328
  2.8 0.0 copy-start.1
  2.8 2.2 %copy-done.1 = bf16[1,512,4096]{2,1,0:T(8,128)(2,1)S(1)} copy-done((bf16[1,512,4096]{2,1,0:T(8,128)(2,1)S(1)}, bf16[1,512,4096]{2,1,0:T(8,128)(2,1)}, u32[]{:S(2)}) %copy-start.1) | copy-done | bytes 4194328
  5.0 0.0 copy-start.2
  5.0 1.4 copy-done.2
  6.4 0.0 copy-start.3
  6.4 1.2 copy-done.3
  7.6 0.0 copy-start.4
  7.6 1.2 copy-done.4
  8.9 0.0 copy-start.5
  8.9 0.9 copy-done.5
  9.8 0.0 copy-start.6
  9.8 0.7 copy-done.6
  10.5 0.0 copy-start.7
  10.5 0.7 copy-done.7
  11.1 0.0 copy-start.8
  11.1 0.7 copy-done.8
  11.8 151.3 %step_pass.1 = (f32[1,7]{1,0:T(1,128)S(1)}, f32[1,512]{1,0:T(1,128)S(1)}, bf16[8,384,256]{2,1,0:T(8,128)(2,1)S(1)}, bf16[384,512]{1,0:T(8,128)(2,1)S(1)}, bf16[8...) custom-call(s32[1,2]{1,0:T(1,128)S(1)} %copy-done.7, s32[2]{0:T(128)S(1)} %copy-done.8, ...), custom_call_target="tpu_custom_call" | custom-call | tf_op jit(solution)/shard_map/step_pass/pallas_call | solution.py:1196
  163.1 6.5 %weight_grads.1 = (f32[2048,512]{1,0:T(8,128)}, f32[2048,128]{1,0:T(8,128)}, f32[2048,128]{1,0:T(8,128)}, f32[512,2048]{1,0:T(8,128)}, f32[1,7]{1,0:T(1,128)}, /*index=5*/f32[1,512]{1,0:T(1,128)}) custom-call(bf16[8,384,256]{2,1,0:T(8,128)(2,1)S(1)} %get-tuple-element.18.normed, bf16[384,512]{1,0:T(8,128)(2,1)S(1)} %get-tuple-element.19.mixture, ...), custom_call_target="tpu_custom_call" | custom-call | tf_op jit(solution)/shard_map/weight_grads/pallas_call | solution.py:1255
Async XLA Ops:
  0.6 2.2 %copy-start = (bf16[1,4096,512]{2,1,0:T(8,128)(2,1)S(1)}, bf16[1,4096,512]{2,1,0:T(8,128)(2,1)}, u32[]{:S(2)}) copy-start(bf16[1,4096,512]{2,1,0:T(8,128)(2,1)} %param.13) | copy-start | bytes 12582916
  2.8 2.2 %copy-start.1 = (bf16[1,512,4096]{2,1,0:T(8,128)(2,1)S(1)}, bf16[1,512,4096]{2,1,0:T(8,128)(2,1)}, u32[]{:S(2)}) copy-start(bf16[1,512,4096]{2,1,0:T(8,128)(2,1)} %param.16) | copy-start | bytes 12582916
  5.0 1.4 copy-start.2
  6.4 1.2 copy-start.3
  7.6 1.2 copy-start.4
  8.9 0.9 copy-start.5
  9.8 0.7 copy-start.6
  10.5 0.7 copy-start.7
  11.1 0.7 copy-start.8

commit v5 on v4

--- a/solution.py
+++ b/solution.py
@@ -1210,7 +1210,12 @@
             collective_id=0, has_side_effects=True, vmem_limit_bytes=36 * 1024 * 1024
         ),
         name="step_pass",
-    )(lengths, positives, entrance, gain, table, wq, wk, wv, wo)
+    )(
+        *[
+            pltpu.with_memory_space_constraint(array, pltpu.HBM)
+            for array in (lengths, positives, entrance, gain, table, wq, wk, wv, wo)
+        ]
+    )
 
 
 def weight_kernel(

time: 170 us -> 161 us (0.947)
  local copies, waits for them, and re-layouts: 11.1 us -> 0 us
  Pallas kernels: 158 us -> 160 us
    unnamed x18 -> x0, local copies, waits for them, and re-layouts: 11.1 us -> none
    pallas_call x1, Pallas kernels: 151 us -> 154 us  [step_pass(): pl.pallas_call(step_kernel, out_shape=(jax.ShapeDtypeStruct((1, WIDTHS),...]
where the time goes in v5:
time: 161 us
  Pallas kernels  160 us (99%)
    pallas_call x1, Pallas kernels, step_pass(): pl.pallas_call(step_kernel, out_shape=(jax.ShapeDtypeStruct((1, WIDTHS),...  154 us
    pallas_call x1, Pallas kernels, weight_grads(): pl.pallas_call(weight_kernel, grid=(share,), in_specs=[vmem] * 6, out_spe...  6.49 us

profile of v5, /device:TPU:0, one launch (start us, length us, event | category | flops | bytes accessed | tf_op | source)
XLA Modules:
  0.0 160.8 jit_solution(15199046010339767409)
XLA Ops:
  0.6 153.7 %step_pass.1 = (f32[1,7]{1,0:T(1,128)S(1)}, f32[1,512]{1,0:T(1,128)S(1)}, bf16[8,384,256]{2,1,0:T(8,128)(2,1)S(1)}, bf16[384,512]{1,0:T(8,128)(2,1)S(1)}, bf16[8...) custom-call(s32[1,2]{1,0:T(1,128)} %lengths.1, s32[2]{0:T(128)} %positives.1, bf16[192,4096]{1,0:T(8,128)(2,1)} %bitcast.11, ...), custom_call_target="tpu_custom_call" | custom-call | tf_op jit(solution)/shard_map/step_pass/pallas_call | solution.py:1196
  154.3 6.5 %weight_grads.1 = (f32[2048,512]{1,0:T(8,128)}, f32[2048,128]{1,0:T(8,128)}, f32[2048,128]{1,0:T(8,128)}, f32[512,2048]{1,0:T(8,128)}, f32[1,7]{1,0:T(1,128)}, /*index=5*/f32[1,512]{1,0:T(1,128)}) custom-call(bf16[8,384,256]{2,1,0:T(8,128)(2,1)S(1)} %get-tuple-element.18.normed, bf16[384,512]{1,0:T(8,128)(2,1)S(1)} %get-tuple-element.19.mixture, ...), custom_call_target="tpu_custom_call" | custom-call | tf_op jit(solution)/shard_map/weight_grads/pallas_call | solution.py:1260

commit v6 on v5

--- a/solution.py
+++ b/solution.py
@@ -18,30 +18,33 @@
 MESH = pl.DeviceIdType.MESH
 ROW_TILE = 16
 SUB = 4
+PIECES = 2
 RELAY, CROSS, TAKE, ATTEND, NEAR, FAR, NEAR_OWN, OWN, FINISH = range(9)
 FORWARD_ORDER = (
-    (RELAY, 0, 0, 1, 2, 3), (CROSS, 0, 0, 2, 1), (TAKE, 0, 0), (RELAY, 1, 0), (CROSS, 0, 3),
-    (TAKE, 0, 2), (RELAY, 1, 1), (TAKE, 0, 1, 3), (RELAY, 1, 2), (ATTEND, 0, 0), (NEAR, 0, 0, 1),
-    (RELAY, 1, 3), (NEAR_OWN, 0, 2, 0), (NEAR, 0, 2), (CROSS, 1, 0), (NEAR, 0, 3), (FAR, 0, 0),
-    (NEAR_OWN, 0, 1), (FAR, 0, 1), (OWN, 0, 0), (CROSS, 1, 1), (TAKE, 1, 0), (CROSS, 1, 2),
-    (FAR, 0, 2, 3), (OWN, 0, 1), (CROSS, 1, 3), (TAKE, 1, 1, 2), (FINISH, 0, 0), (TAKE, 1, 3),
-    (ATTEND, 1, 0), (FINISH, 0, 1), (NEAR, 1, 0), (NEAR_OWN, 0, 3), (OWN, 0, 2), (NEAR, 1, 1),
-    (FINISH, 0, 2), (NEAR_OWN, 1, 0), (FAR, 1, 0), (OWN, 0, 3), (FINISH, 0, 3), (NEAR, 1, 2, 3),
-    (FAR, 1, 1), (NEAR_OWN, 1, 2), (FAR, 1, 2), (NEAR_OWN, 1, 1), (FAR, 1, 3), (OWN, 1, 0),
-    (FINISH, 1, 0), (NEAR_OWN, 1, 3), (OWN, 1, 1), (FINISH, 1, 1), (OWN, 1, 2, 3),
-    (FINISH, 1, 2, 3),
+    (RELAY, 0, 0, 1, 2, 3, 4, 5, 6, 7), (CROSS, 0, 0, 1, 4, 5, 2, 3), (TAKE, 0, 0),
+    (RELAY, 1, 0, 1), (CROSS, 0, 6, 7), (TAKE, 0, 2), (RELAY, 1, 2, 3), (TAKE, 0, 1, 3),
+    (RELAY, 1, 4, 5), (ATTEND, 0, 0), (NEAR, 0, 0, 1), (RELAY, 1, 6, 7), (NEAR_OWN, 0, 2, 0),
+    (NEAR, 0, 2), (CROSS, 1, 0, 1), (NEAR, 0, 3), (FAR, 0, 0), (NEAR_OWN, 0, 1), (FAR, 0, 1),
+    (OWN, 0, 0), (CROSS, 1, 2, 3), (TAKE, 1, 0), (CROSS, 1, 4, 5), (FAR, 0, 2, 3), (OWN, 0, 1),
+    (CROSS, 1, 6, 7), (TAKE, 1, 1, 2), (FINISH, 0, 0, 1), (TAKE, 1, 3), (ATTEND, 1, 0),
+    (FINISH, 0, 2, 3), (NEAR, 1, 0), (NEAR_OWN, 0, 3), (OWN, 0, 2), (NEAR, 1, 1),
+    (FINISH, 0, 4, 5), (NEAR_OWN, 1, 0), (FAR, 1, 0), (OWN, 0, 3), (FINISH, 0, 6, 7),
+    (NEAR, 1, 2, 3), (FAR, 1, 1), (NEAR_OWN, 1, 2), (FAR, 1, 2), (NEAR_OWN, 1, 1), (FAR, 1, 3),
+    (OWN, 1, 0), (FINISH, 1, 0, 1), (NEAR_OWN, 1, 3), (OWN, 1, 1), (FINISH, 1, 2, 3),
+    (OWN, 1, 2, 3), (FINISH, 1, 4, 5, 6, 7),
 )
 BACKWARD_ORDER = (
-    (RELAY, 0, 0, 1, 2, 3), (CROSS, 0, 0, 1), (TAKE, 0, 0), (CROSS, 0, 2), (TAKE, 0, 1),
-    (CROSS, 0, 3), (TAKE, 0, 2, 3), (ATTEND, 0, 0), (NEAR, 0, 0), (NEAR_OWN, 0, 0),
-    (NEAR, 0, 1, 2), (FAR, 0, 0), (NEAR, 0, 3), (FAR, 0, 1, 2), (NEAR_OWN, 0, 2, 1), (OWN, 0, 0),
-    (FAR, 0, 3), (FINISH, 0, 0), (RELAY, 1, 0), (OWN, 0, 2, 1), (RELAY, 1, 1), (FINISH, 0, 1),
-    (NEAR_OWN, 0, 3), (RELAY, 1, 2), (FINISH, 0, 2), (OWN, 0, 3), (RELAY, 1, 3), (FINISH, 0, 3),
-    (CROSS, 1, 0, 1), (TAKE, 1, 0), (CROSS, 1, 2), (TAKE, 1, 1), (CROSS, 1, 3), (TAKE, 1, 2, 3),
+    (RELAY, 0, 0, 1, 2, 3, 4, 5, 6, 7), (CROSS, 0, 0, 1, 2, 3), (TAKE, 0, 0), (CROSS, 0, 4, 5),
+    (TAKE, 0, 1), (CROSS, 0, 6, 7), (TAKE, 0, 2, 3), (ATTEND, 0, 0), (NEAR, 0, 0),
+    (NEAR_OWN, 0, 0), (NEAR, 0, 1, 2), (FAR, 0, 0), (NEAR, 0, 3), (FAR, 0, 1, 2),
+    (NEAR_OWN, 0, 2, 1), (OWN, 0, 0), (FAR, 0, 3), (FINISH, 0, 0, 1), (RELAY, 1, 0, 1),
+    (OWN, 0, 2, 1), (RELAY, 1, 2, 3), (FINISH, 0, 2, 3), (NEAR_OWN, 0, 3), (RELAY, 1, 4, 5),
+    (FINISH, 0, 4, 5), (OWN, 0, 3), (RELAY, 1, 6, 7), (FINISH, 0, 6, 7), (CROSS, 1, 0, 1, 2, 3),
+    (TAKE, 1, 0), (CROSS, 1, 4, 5), (TAKE, 1, 1), (CROSS, 1, 6, 7), (TAKE, 1, 2, 3),
     (ATTEND, 1, 0), (NEAR, 1, 0, 1), (NEAR_OWN, 1, 0), (NEAR, 1, 3), (FAR, 1, 0), (NEAR, 1, 2),
-    (FAR, 1, 1), (OWN, 1, 0), (NEAR_OWN, 1, 1), (FAR, 1, 2, 3), (NEAR_OWN, 1, 2), (FINISH, 1, 0),
-    (OWN, 1, 1), (NEAR_OWN, 1, 3), (FINISH, 1, 1), (OWN, 1, 2), (FINISH, 1, 2), (OWN, 1, 3),
-    (FINISH, 1, 3),
+    (FAR, 1, 1), (OWN, 1, 0), (NEAR_OWN, 1, 1), (FAR, 1, 2, 3), (NEAR_OWN, 1, 2),
+    (FINISH, 1, 0, 1), (OWN, 1, 1), (NEAR_OWN, 1, 3), (FINISH, 1, 2, 3), (OWN, 1, 2),
+    (FINISH, 1, 4, 5), (OWN, 1, 3), (FINISH, 1, 6, 7),
 )
 F32 = jnp.float32
 BF16 = jnp.bfloat16
@@ -116,42 +119,43 @@
         self.relay, self.far, self.near = relay, far, near
         self.group = group
 
-    def at(self, block):
-        return self.buf.at[self.group * 4 * SUB + block]
-
-    def relay_copy(self, step, block):
-        slot = self.group * SUB + step
-        return send(self.at(block), self.at(block), self.relay, slot, section=self.place.here)
-
-    def near_copy(self, slot, block):
-        slot = self.group * 2 * SUB + slot
-        return send(self.at(block), self.at(block), self.near, slot, mp=self.place.near)
-
-    def far_copy(self, step, block):
-        slot = self.group * SUB + step
-        return send(self.at(block), self.at(block), self.far, slot, mp=self.place.far)
+    def copy(self, sems, first, step, block, **device):
+        rows = self.buf.shape[1] // PIECES
+        slot = self.group * 4 * SUB + block + step // PIECES
+        piece = self.buf.at[slot, pl.ds(step % PIECES * rows, rows)]
+        return send(piece, piece, sems, first * SUB * PIECES + step, **device)
+
+    def relay_copy(self, step):
+        own = self.place.quarter(0, 0)
+        return self.copy(self.relay, self.group, step, own, section=self.place.here)
+
+    def far_copy(self, step, flip):
+        block = self.place.quarter(0, flip)
+        return self.copy(self.far, self.group, step, block, mp=self.place.far)
+
+    def near_copy(self, step, low, high):
+        block = self.place.quarter(low, high)
+        return self.copy(self.near, self.group * 2 + high, step, block, mp=self.place.near)
 
     def relay_step(self, step):
-        block = self.place.quarter(0, 0) + step
-        self.relay_copy(step, block).wait_recv()
-        self.far_copy(step, block).start()
-        self.near_copy(step, block).start()
+        self.relay_copy(step).wait_recv()
+        self.far_copy(step, 0).start()
+        self.near_copy(step, 0, 0).start()
 
     def cross_step(self, step):
-        block = self.place.quarter(0, 1) + step
-        self.far_copy(step, block).wait_recv()
-        self.near_copy(SUB + step, block).start()
-
-    def settle(self, step):
-        self.near_copy(step, self.place.quarter(1, 0) + step).wait_recv()
-        self.near_copy(SUB + step, self.place.quarter(1, 1) + step).wait_recv()
+        self.far_copy(step, 1).wait_recv()
+        self.near_copy(step, 0, 1).start()
+
+    def settle(self, block):
+        for step in range(block * PIECES, (block + 1) * PIECES):
+            self.near_copy(step, 1, 0).wait_recv()
+            self.near_copy(step, 1, 1).wait_recv()
 
     def drain(self):
-        own, other = self.place.quarter(0, 0), self.place.quarter(0, 1)
-        for step in range(SUB):
-            self.far_copy(step, own + step).wait_send()
-            self.near_copy(step, own + step).wait_send()
-            self.near_copy(SUB + step, other + step).wait_send()
+        for step in range(SUB * PIECES):
+            self.far_copy(step, 0).wait_send()
+            self.near_copy(step, 0, 0).wait_send()
+            self.near_copy(step, 0, 1).wait_send()
 
 
 class StreamOut:
@@ -163,66 +167,83 @@
         )
         self.relay_sems, self.far_sems, self.near_sems = relay, far, near
 
-    def near_copy(self, slot):
+    def copy(self, source, target, sems, slot, piece, **device):
+        rows = source.shape[1] // PIECES
+        span = pl.ds(piece * rows, rows)
+        return send(
+            source.at[slot, span], target[0].at[target[1], span], sems, slot * PIECES + piece, **device
+        )
+
+    def near_copies(self, slot):
         slot = self.group * 2 * SUB + slot
-        return send(
-            self.near_send.at[slot], self.near_got.at[slot], self.near_sems, slot, mp=self.place.near
-        )
+        target = (self.near_got, slot)
+        return [
+            self.copy(self.near_send, target, self.near_sems, slot, piece, mp=self.place.near)
+            for piece in range(PIECES)
+        ]
 
     def far_copy(self, step):
-        slot = self.group * SUB + step
-        return send(
-            self.far_send.at[slot], self.far_got.at[slot], self.far_sems, slot, mp=self.place.far
+        slot = self.group * SUB + step // PIECES
+        target = (self.far_got, slot)
+        return self.copy(
+            self.far_send, target, self.far_sems, slot, step % PIECES, mp=self.place.far
         )
 
     def relay_copy(self, step):
-        slot = self.group * SUB + step
         place = self.place
-        return send(
-            self.relay_send.at[slot],
-            self.dest.at[self.group * 4 * SUB + place.quarter(0, 0) + step],
+        slot = self.group * SUB + step // PIECES
+        target = (self.dest, self.group * 4 * SUB + place.quarter(0, 0) + step // PIECES)
+        return self.copy(
+            self.relay_send,
+            target,
             self.relay_sems,
             slot,
+            step % PIECES,
             section=place.here + place.direction,
         )
 
-    def near(self, flip, step):
-        place = self.place
-        slot = (1 - place.high if flip else place.high) * SUB + step
-        value = self.part_of(self.group, place.quarter(1, flip) + step)
+    def part(self, kind, step):
+        flips = {NEAR: (1, 1), NEAR_OWN: (1, 0), FAR: (0, 1), OWN: (0, 0)}[kind]
+        return self.part_of(self.group, self.place.quarter(*flips) + step)
+
+    def near(self, flip, step, value):
+        slot = (1 - self.place.high if flip else self.place.high) * SUB + step
         self.near_send[self.group * 2 * SUB + slot] = value.astype(BF16)
-        self.near_copy(slot).start()
+        for copy in self.near_copies(slot):
+            copy.start()
 
     def arrived(self, slot):
-        self.near_copy(slot).wait_recv()
+        for copy in self.near_copies(slot):
+            copy.wait_recv()
         return self.near_got[self.group * 2 * SUB + slot].astype(F32)
 
-    def far(self, step):
-        place = self.place
-        value = self.part_of(self.group, place.quarter(0, 1) + step)
-        value = value + self.arrived((1 - place.high) * SUB + step)
+    def far(self, step, value):
+        value = value + self.arrived((1 - self.place.high) * SUB + step)
         self.far_send[self.group * SUB + step] = value.astype(BF16)
-        self.far_copy(step).start()
-
-    def own(self, step):
-        place = self.place
-        value = self.part_of(self.group, place.quarter(0, 0) + step)
-        self.keep[self.group * SUB + step] = value + self.arrived(place.high * SUB + step)
+        for piece in range(PIECES):
+            self.far_copy(step * PIECES + piece).start()
+
+    def own(self, step, value):
+        value = value + self.arrived(self.place.high * SUB + step)
+        self.keep[self.group * SUB + step] = value
 
     def finish(self, step):
-        slot = self.group * SUB + step
-        block = self.place.quarter(0, 0) + step
+        slot = self.group * SUB + step // PIECES
+        block = self.place.quarter(0, 0) + step // PIECES
+        rows = self.keep.shape[1] // PIECES
+        inner = slice(step % PIECES * rows, (step % PIECES + 1) * rows)
         self.far_copy(step).wait_recv()
-        value = self.keep[slot] + self.far_got[slot].astype(F32)
-        self.relay_send[slot] = self.finish_of(self.group, block, value)
+        value = self.keep[slot, inner, :] + self.far_got[slot, inner, :].astype(F32)
+        self.relay_send[slot, inner, :] = self.finish_of(self.group, block, value, inner)
         self.relay_copy(step).start()
 
     def drain(self):
-        for step in range(SUB):
+        for step in range(SUB * PIECES):
             self.far_copy(step).wait_send()
             self.relay_copy(step).wait_send()
         for slot in range(2 * SUB):
-            self.near_copy(slot).wait_send()
+            for copy in self.near_copies(slot):
+                copy.wait_send()
 
 
 def run_pass(order, ins, outs, has_source, has_target, consume, attend, prepare, rest):
@@ -234,9 +255,12 @@
         for quarter in range(4):
             consume(group, quarter * SUB + step)
 
+    prepared = set()
+
     def finish(group, step):
-        if step == 0:
+        if group not in prepared:
             prepare(group)
+            prepared.add(group)
         outs[group].finish(step)
 
     receive = {
@@ -244,11 +268,10 @@
         CROSS: lambda group, step: ins[group].cross_step(step),
     }
     produce = {
-        NEAR: lambda group, step: outs[group].near(1, step),
-        NEAR_OWN: lambda group, step: outs[group].near(0, step),
-        FAR: lambda group, step: outs[group].far(step),
-        OWN: lambda group, step: outs[group].own(step),
-        FINISH: finish,
+        NEAR: lambda group, step, value: outs[group].near(1, step, value),
+        NEAR_OWN: lambda group, step, value: outs[group].near(0, step, value),
+        FAR: lambda group, step, value: outs[group].far(step, value),
+        OWN: lambda group, step, value: outs[group].own(step, value),
     }
     for kind, group, *steps in order:
         if kind == ATTEND:
@@ -258,13 +281,26 @@
         elif kind == TAKE:
             for step in steps:
                 take(group, step)
-        else:
-            action = receive.get(kind) or produce[kind]
-
-            @pl.when(has_source if kind in receive else has_target)
-            def _(group=group, steps=steps, action=action):
+        elif kind in receive:
+
+            @pl.when(has_source)
+            def _(group=group, steps=steps, action=receive[kind]):
                 for step in steps:
                     action(group, step)
+
+        elif kind == FINISH:
+
+            @pl.when(has_target)
+            def _(group=group, steps=steps):
+                for step in steps:
+                    finish(group, step)
+
+        else:
+
+            @pl.when(has_target)
+            def _(group=group, steps=steps, kind=kind):
+                for step in steps:
+                    produce[kind](group, step, outs[group].part(kind, step))
 
 
 def drain_pass(ins, outs, has_source, has_target):
@@ -480,11 +516,13 @@
     wo,
     losses_out,
     gain_out,
-    normed_all,
-    mixture_all,
+    normed_turned,
+    mixture_turned,
     outer_all,
     heads_all,
     hidden,
+    normed_all,
+    mixture_all,
     *scratch,
 ):
     r = Scratch(*scratch)
@@ -496,7 +534,7 @@
     pair_count = lengths.shape[0]
     seq_count = 2 * pair_count
     length = rows // pair_count
-    query_cols, kv_cols = wq.shape[1], wk.shape[1]
+    query_cols, kv_cols = wq.shape[3], wk.shape[3]
     groups = query_cols // HEAD
     dp_me, mp_me = lax.axis_index("dp"), lax.axis_index("mp")
     dp_count, mp_count = lax.axis_size("dp"), lax.axis_size("mp")
@@ -532,12 +570,21 @@
     def valid_of(seq):
         return jnp.where(spot < count_of(seq), 1.0, 0.0)
 
-    loads = [
-        pltpu.make_async_copy(wq, head_w.at[:, :query_cols], r.load_sem.at[0]),
-        pltpu.make_async_copy(wk, head_w.at[:, query_cols : query_cols + kv_cols], r.load_sem.at[1]),
-        pltpu.make_async_copy(wv, head_w.at[:, query_cols + kv_cols :], r.load_sem.at[2]),
-        pltpu.make_async_copy(wo, out_w, r.load_sem.at[3]),
-    ]
+    def load(chunk):
+        copies, start = [], 0
+        for index, weight in enumerate((wq, wk, wv)):
+            columns = pl.ds(start, weight.shape[3])
+            copies.append(
+                pltpu.make_async_copy(
+                    weight.at[:, chunk],
+                    head_w.at[:, chunk, :, columns],
+                    r.load_sem.at[3 * chunk + index],
+                )
+            )
+            start += weight.shape[3]
+        return copies
+
+    load_out = pltpu.make_async_copy(wo, out_w, r.load_sem.at[3 * SUB])
 
     def enter(group, block):
         slot = group * blocks + block
@@ -547,14 +594,17 @@
             r.enter_sem.at[slot],
         )
 
+    for chunk in range(SUB):
+        for copy in load(chunk):
+            copy.start()
+
     @pl.when(jnp.logical_not(forth.has_source))
     def _():
         for group in range(2):
             for block in range(blocks):
                 enter(group, block).start()
 
-    for load in loads:
-        load.start()
+    load_out.start()
     barrier = pltpu.get_barrier_semaphore()
     for shift in range(1, members):
         to_dp, to_mp, _ = peer(shift)
@@ -595,14 +645,15 @@
         inside = jnp.logical_and(column >= seq * length, column < seq * length + count_of(seq))
         picks = jnp.where(jnp.logical_and(line == seq % pair_count, inside), 1.0, picks)
     r.pool_ref[...] = picks.astype(BF16)
-    for load in loads[:3]:
-        load.wait()
     expected = (
         members - 1 + forth.has_source.astype(jnp.int32) + forth.has_target.astype(jnp.int32)
     )
 
     @pl.when(forth.has_source)
     def _():
+        for chunk in range(SUB):
+            for copy in load(chunk):
+                copy.wait()
         pl.semaphore_wait(barrier, expected)
 
     def gain_at(block):
@@ -617,6 +668,9 @@
         @pl.when(jnp.logical_not(forth.has_source))
         def _():
             enter(group, block).wait()
+            if group == 0 and block < SUB:
+                for copy in load(block):
+                    copy.wait()
 
         value = hidden[slot].astype(F32)
         span = span_of(group)
@@ -627,7 +681,7 @@
             )
         acc[span, :] += jnp.dot(
             (value * gain_at(block)).astype(BF16),
-            head_w[rows_at(block * width, width), :],
+            head_w[block // SUB, block % SUB],
             preferred_element_type=F32,
         )
 
@@ -671,7 +725,7 @@
             def _():
                 pl.semaphore_wait(barrier, expected)
 
-            loads[3].wait()
+            load_out.wait()
 
     first = (mp_me == 0).astype(F32)
     pooled = r.pooled
@@ -714,8 +768,8 @@
     def part(group, block):
         return jnp.dot(mixture[span_of(group), :], out_columns(block), preferred_element_type=F32)
 
-    def finish(group, block, total):
-        return (hidden[group * blocks + block].astype(F32) + total).astype(BF16)
+    def finish(group, block, total, inner):
+        return (hidden[group * blocks + block, inner, :].astype(F32) + total).astype(BF16)
 
     ins = [
         StreamIn(
@@ -743,7 +797,15 @@
         for group in range(2)
     ]
     run_pass(
-        FORWARD_ORDER, ins, outs, forth.has_source, forth.has_target, consume, attend, lambda group: None, send_pooled
+        FORWARD_ORDER,
+        ins,
+        outs,
+        forth.has_source,
+        forth.has_target,
+        consume,
+        attend,
+        lambda group: None,
+        send_pooled,
     )
 
     @pl.when(forth.has_target)
@@ -814,6 +876,21 @@
             lax.fori_loop(0, blocks, normed_block, 0, unroll=2)
             for shift in range(1, dp_count):
                 rows_copy(mixture_all, mixture_sems, shift, group, True).start()
+
+    def turn_over():
+        for group in range(2):
+            for shift in range(1, dp_count):
+                member = lax.rem(dp_me + shift, dp_count)
+                rows_copy(mixture_all, mixture_sems, shift, group, False).wait_recv()
+                for step in range(share):
+                    from_member(normed_all, normed_sems, member, group, step).wait_recv()
+
+        def turn(step, carry):
+            normed_turned[step] = normed_all[step].T
+            return carry
+
+        lax.fori_loop(0, share, turn, 0)
+        mixture_turned[...] = mixture_all[...].T
 
     pl.when(back.has_source)(hand_out_normed)
     for group in range(2):
@@ -851,6 +928,9 @@
     for p in range(pairs):
         slopes[2 * p] = query_slopes[p : p + 1]
         slopes[2 * p + 1] = passage_slopes[p : p + 1]
+
+    waits_long = back.here < back.count - 2
+    pl.when(waits_long)(turn_over)
 
     grad_in, mix_grad = r.grad_in, r.mix_grad
 
@@ -925,7 +1005,7 @@
 
     def part_back(group, block):
         span = span_of(group)
-        value = contract_last(head_grads[span, :], head_w[rows_at(block * width, width), :])
+        value = contract_last(head_grads[span, :], head_w[block // SUB, lax.rem(block, SUB)])
         scaled = value * (hidden[group * blocks + block].astype(F32) * r.inv_ref[span, :])
         r.gain_part[:, lanes_at(block * width, width)] += jnp.sum(scaled, axis=0, keepdims=True)
         return value
@@ -945,10 +1025,10 @@
             * (1.0 / width_all)
         )
 
-    def finish_back(group, block, total):
-        span = span_of(group)
-        value = upstream(group, block) + total * gain_at(block) * r.inv_ref[span, :]
-        pulled = hidden[group * blocks + block].astype(F32) * r.pull_ref[span, :]
+    def finish_back(group, block, total, inner):
+        span = slice(group * rows + inner.start, group * rows + inner.stop)
+        value = upstream(group, block)[inner] + total * gain_at(block) * r.inv_ref[span, :]
+        pulled = hidden[group * blocks + block, inner, :].astype(F32) * r.pull_ref[span, :]
         return (value - pulled).astype(BF16)
 
     def gain_only(group):
@@ -956,7 +1036,7 @@
             part_back(group, block)
             return carry
 
-        lax.fori_loop(0, blocks, body, 0, unroll=2)
+        lax.fori_loop(0, blocks, body, 0, unroll=4)
 
     ins_back = [
         StreamIn(
@@ -996,6 +1076,7 @@
     )
 
     pl.when(jnp.logical_not(back.has_source))(hand_out_normed)
+    pl.when(jnp.logical_not(waits_long))(turn_over)
 
     def pass_on(member, group, step):
         piece = outer_all.at[step, member_rows(member, group)]
@@ -1070,7 +1151,6 @@
         for shift in range(1, dp_count):
             rows_copy(mixture_all, mixture_sems, shift, group, True).wait_send()
             rows_copy(heads_all, heads_sems, shift, group, True).wait_send()
-            rows_copy(mixture_all, mixture_sems, shift, group, False).wait_recv()
             rows_copy(heads_all, heads_sems, shift, group, False).wait_recv()
 
         def drain(block, carry, group=group):
@@ -1089,8 +1169,6 @@
         lax.fori_loop(0, blocks, drain, 0)
         for shift in range(1, dp_count):
             member = lax.rem(dp_me + shift, dp_count)
-            for step in range(share):
-                from_member(normed_all, normed_sems, member, group, step).wait_recv()
             for pair in range(share // 2):
                 pass_on(member, group, 2 * pair + forth.low).wait_send()
 
@@ -1109,10 +1187,11 @@
     stacked = query_cols // HEAD * length
     row_pad = -(-(rows // 2) // 128) * 128
     pool_rows = -(-seq_count // 16) * 16
+    head_weights = [weight.reshape(mp_count, SUB, width, -1) for weight in (wq, wk, wv)]
     dma = pltpu.SemaphoreType.DMA
     block = (rows // 2, width)
     shapes = dict(
-        head_w=((width_all, head_cols), BF16),
+        head_w=((mp_count, SUB, width, head_cols), BF16),
         out_w=(wo.shape, BF16),
         acc=((rows, head_cols), F32),
         squares=((rows, 128), F32),
@@ -1147,7 +1226,7 @@
         keep_b=((2 * SUB, *block), F32),
     )
     counts = dict(
-        load_sem=(4,),
+        load_sem=(3 * SUB + 1,),
         enter_sem=(2 * blocks,),
         pool_s=(2 * members,),
         pool_r=(2 * members,),
@@ -1165,26 +1244,26 @@
         dots_r=(2 * mp_count,),
         gain_s=(members,),
         gain_r=(members,),
-        relay_s=(2 * SUB,),
-        in_far_s=(2 * SUB,),
-        out_far_s=(2 * SUB,),
-        in_near_s=(4 * SUB,),
-        out_near_s=(4 * SUB,),
-        relay_r=(2 * SUB,),
-        in_far_r=(2 * SUB,),
-        out_far_r=(2 * SUB,),
-        in_near_r=(4 * SUB,),
-        out_near_r=(4 * SUB,),
-        relay_sb=(2 * SUB,),
-        in_far_sb=(2 * SUB,),
-        out_far_sb=(2 * SUB,),
-        in_near_sb=(4 * SUB,),
-        out_near_sb=(4 * SUB,),
-        relay_rb=(2 * SUB,),
-        in_far_rb=(2 * SUB,),
-        out_far_rb=(2 * SUB,),
-        in_near_rb=(4 * SUB,),
-        out_near_rb=(4 * SUB,),
+        relay_s=(2 * SUB * PIECES,),
+        in_far_s=(2 * SUB * PIECES,),
+        out_far_s=(2 * SUB * PIECES,),
+        in_near_s=(4 * SUB * PIECES,),
+        out_near_s=(4 * SUB * PIECES,),
+        relay_r=(2 * SUB * PIECES,),
+        in_far_r=(2 * SUB * PIECES,),
+        out_far_r=(2 * SUB * PIECES,),
+        in_near_r=(4 * SUB * PIECES,),
+        out_near_r=(4 * SUB * PIECES,),
+        relay_sb=(2 * SUB * PIECES,),
+        in_far_sb=(2 * SUB * PIECES,),
+        out_far_sb=(2 * SUB * PIECES,),
+        in_near_sb=(4 * SUB * PIECES,),
+        out_near_sb=(4 * SUB * PIECES,),
+        relay_rb=(2 * SUB * PIECES,),
+        in_far_rb=(2 * SUB * PIECES,),
+        out_far_rb=(2 * SUB * PIECES,),
+        in_near_rb=(4 * SUB * PIECES,),
+        out_near_rb=(4 * SUB * PIECES,),
     )
     scratch = Scratch(
         **{name: pltpu.VMEM(*shape) for name, shape in shapes.items()},
@@ -1198,14 +1277,19 @@
         out_shape=(
             jax.ShapeDtypeStruct((1, WIDTHS), F32),
             jax.ShapeDtypeStruct((1, width_all // members), F32),
-            jax.ShapeDtypeStruct((share, dp_count * rows, width), BF16),
-            jax.ShapeDtypeStruct((dp_count * rows, query_cols), BF16),
+            jax.ShapeDtypeStruct((share, width, dp_count * rows), BF16),
+            jax.ShapeDtypeStruct((query_cols, dp_count * rows), BF16),
             jax.ShapeDtypeStruct((share, dp_count * rows, width), BF16),
             jax.ShapeDtypeStruct((dp_count * rows, head_cols), BF16),
         ),
         in_specs=[smem, smem, hbm, vmem, vmem, hbm, hbm, hbm, hbm],
         out_specs=(vmem,) * 6,
-        scratch_shapes=[pltpu.VMEM((2 * blocks, *block), BF16)] + list(scratch),
+        scratch_shapes=[
+            pltpu.VMEM((2 * blocks, *block), BF16),
+            pltpu.VMEM((share, dp_count * rows, width), BF16),
+            pltpu.VMEM((dp_count * rows, query_cols), BF16),
+            *scratch,
+        ],
         compiler_params=pltpu.CompilerParams(
             collective_id=0, has_side_effects=True, vmem_limit_bytes=36 * 1024 * 1024
         ),
@@ -1213,7 +1297,7 @@
     )(
         *[
             pltpu.with_memory_space_constraint(array, pltpu.HBM)
-            for array in (lengths, positives, entrance, gain, table, wq, wk, wv, wo)
+            for array in (lengths, positives, entrance, gain, table, *head_weights, wo)
         ]
     )
 
@@ -1231,26 +1315,24 @@
     out_grad,
     losses_out,
     gain_out,
-    turned,
 ):
     query_cols, kv_cols = query_grad.shape[1], key_grad.shape[1]
 
     @pl.when(pl.program_id(0) == 0)
     def _():
-        turned[...] = mixture[...].T
         losses_out[...] = losses[...]
         gain_out[...] = gain_share[...]
 
     step = pl.program_id(0)
-    product = contract_rows(normed[step], heads[...])
+    product = jnp.dot(normed[step], heads[...], preferred_element_type=F32)
     query_grad[...] = product[:, :query_cols]
     key_grad[...] = product[:, query_cols : query_cols + kv_cols]
     value_grad[...] = product[:, query_cols + kv_cols :]
-    out_grad[...] = jnp.dot(turned[...], outer[step], preferred_element_type=F32)
+    out_grad[...] = jnp.dot(mixture[...], outer[step], preferred_element_type=F32)
 
 
 def weight_grads(normed, mixture, outer, heads, losses, gain_share, query_cols, kv_cols):
-    share, rows, width = normed.shape
+    share, width, _ = normed.shape
     columns = share * width
     vmem = pl.BlockSpec(memory_space=pltpu.VMEM)
 
@@ -1277,7 +1359,6 @@
             jax.ShapeDtypeStruct(losses.shape, F32),
             jax.ShapeDtypeStruct(gain_share.shape, F32),
         ),
-        scratch_shapes=[pltpu.VMEM((query_cols, rows), BF16)],
         compiler_params=pltpu.CompilerParams(
             dimension_semantics=("arbitrary",), vmem_limit_bytes=16 * 1024 * 1024
         ),

time: 161 us -> 159 us (0.988)
  no operation moved by 1% of the time
where the time goes in v6:
time: 159 us
  Pallas kernels  159 us (100%)
    pallas_call x1, Pallas kernels, step_pass(): pl.pallas_call(step_kernel, out_shape=(jax.ShapeDtypeStruct((1, WIDTHS),...  152 us
    pallas_call x1, Pallas kernels, weight_grads(): pl.pallas_call(weight_kernel, grid=(share,), in_specs=[vmem] * 6, out_spe...  6.13 us

profile of v6, /device:TPU:0, one launch (start us, length us, event | category | flops | bytes accessed | tf_op | source)
XLA Modules:
  0.0 159.1 jit_solution(173956698818501686)
XLA Ops:
  0.6 152.4 %step_pass.1 = (f32[1,7]{1,0:T(1,128)S(1)}, f32[1,512]{1,0:T(1,128)S(1)}, bf16[8,256,384]{2,1,0:T(8,128)(2,1)S(1)}, bf16[512,384]{1,0:T(8,128)(2,1)S(1)}, bf16[8...) custom-call(s32[1,2]{1,0:T(1,128)} %lengths.1, s32[2]{0:T(128)} %positives.1, bf16[192,4096]{1,0:T(8,128)(2,1)} %bitcast.11, ...), custom_call_target="tpu_custom_call" | custom-call | tf_op jit(solution)/shard_map/step_pass/pallas_call | solution.py:1275
  153.0 6.1 %weight_grads.1 = (f32[2048,512]{1,0:T(8,128)}, f32[2048,128]{1,0:T(8,128)}, f32[2048,128]{1,0:T(8,128)}, f32[512,2048]{1,0:T(8,128)}, f32[1,7]{1,0:T(1,128)}, /*index=5*/f32[1,512]{1,0:T(1,128)}) custom-call(bf16[8,256,384]{2,1,0:T(8,128)(2,1)S(1)} %get-tuple-element.18.normed, bf16[512,384]{1,0:T(8,128)(2,1)S(1)} %get-tuple-element.19.mixture, ...), custom_call_target="tpu_custom_call" | custom-call | tf_op jit(solution)/shard_map/weight_grads/pallas_call | solution.py:1342

commit v7 on v6

--- a/solution.py
+++ b/solution.py
@@ -1323,12 +1323,15 @@
         losses_out[...] = losses[...]
         gain_out[...] = gain_share[...]
 
-    step = pl.program_id(0)
-    product = jnp.dot(normed[step], heads[...], preferred_element_type=F32)
-    query_grad[...] = product[:, :query_cols]
-    key_grad[...] = product[:, query_cols : query_cols + kv_cols]
-    value_grad[...] = product[:, query_cols + kv_cols :]
-    out_grad[...] = jnp.dot(mixture[...], outer[step], preferred_element_type=F32)
+    width = normed.shape[1]
+    for half in range(2):
+        step = pl.program_id(0) * 2 + half
+        span = slice(half * width, (half + 1) * width)
+        product = jnp.dot(normed[step], heads[...], preferred_element_type=F32)
+        query_grad[span, :] = product[:, :query_cols]
+        key_grad[span, :] = product[:, query_cols : query_cols + kv_cols]
+        value_grad[span, :] = product[:, query_cols + kv_cols :]
+        out_grad[:, span] = jnp.dot(mixture[...], outer[step], preferred_element_type=F32)
 
 
 def weight_grads(normed, mixture, outer, heads, losses, gain_share, query_cols, kv_cols):
@@ -1337,17 +1340,17 @@
     vmem = pl.BlockSpec(memory_space=pltpu.VMEM)
 
     def tall(cols):
-        return pl.BlockSpec((width, cols), lambda step: (step, 0))
+        return pl.BlockSpec((2 * width, cols), lambda step: (step, 0))
 
     return pl.pallas_call(
         weight_kernel,
-        grid=(share,),
+        grid=(share // 2,),
         in_specs=[vmem] * 6,
         out_specs=(
             tall(query_cols),
             tall(kv_cols),
             tall(kv_cols),
-            pl.BlockSpec((query_cols, width), lambda step: (0, step)),
+            pl.BlockSpec((query_cols, 2 * width), lambda step: (0, step)),
             vmem,
             vmem,
         ),

time: 159 us -> 158 us (level)
  no operation moved by 1% of the time
where the time goes in v7:
time: 158 us
  Pallas kernels  158 us (100%)
    pallas_call x1, Pallas kernels, step_pass(): pl.pallas_call(step_kernel, out_shape=(jax.ShapeDtypeStruct((1, WIDTHS),...  152 us
    pallas_call x1, Pallas kernels, weight_grads(): pl.pallas_call(weight_kernel, grid=(share // 2,), in_specs=[vmem] * 6, ou...  5.27 us

profile of v7, /device:TPU:0, one launch (start us, length us, event | category | flops | bytes accessed | tf_op | source)
XLA Modules:
  0.0 158.3 jit_solution(15900193149378595012)
XLA Ops:
  0.6 152.4 %step_pass.1 = (f32[1,7]{1,0:T(1,128)S(1)}, f32[1,512]{1,0:T(1,128)S(1)}, bf16[8,256,384]{2,1,0:T(8,128)(2,1)S(1)}, bf16[512,384]{1,0:T(8,128)(2,1)S(1)}, bf16[8...) custom-call(s32[1,2]{1,0:T(1,128)} %lengths.1, s32[2]{0:T(128)} %positives.1, bf16[192,4096]{1,0:T(8,128)(2,1)} %bitcast.11, ...), custom_call_target="tpu_custom_call" | custom-call | tf_op jit(solution)/shard_map/step_pass/pallas_call | solution.py:1275
  153.0 5.3 %weight_grads.1 = (f32[2048,512]{1,0:T(8,128)}, f32[2048,128]{1,0:T(8,128)}, f32[2048,128]{1,0:T(8,128)}, f32[512,2048]{1,0:T(8,128)}, f32[1,7]{1,0:T(1,128)}, /*index=5*/f32[1,512]{1,0:T(1,128)}) custom-call(bf16[8,256,384]{2,1,0:T(8,128)(2,1)S(1)} %get-tuple-element.18.normed, bf16[512,384]{1,0:T(8,128)(2,1)S(1)} %get-tuple-element.19.mixture, ...), custom_call_target="tpu_custom_call" | custom-call | tf_op jit(solution)/shard_map/weight_grads/pallas_call | solution.py:1345
